TPU v7x, 32 devices: a whole 2x2x4 slice. The times are simulated.
32 devices in a mesh: rep: 16 (over z, y, core), grp: 2 (over x).
Axes of the slice: x: 2, y: 2, z: 4, core: 2. Of those that a mesh axis runs over, the one named last changes fastest.
Arguments:
- tokens: bfloat16 [24576, 768], P(('rep', 'grp')), may hold values from -6 to 6
- query_weight: bfloat16 [1536, 768], P('grp'), may hold values from -0.21875 to 0.21875
- key_weight: bfloat16 [256, 768], P('grp'), may hold values from -0.21875 to 0.21875
- value_weight: bfloat16 [256, 768], P('grp'), may hold values from -0.21875 to 0.21875
- query_bias: bfloat16 [1536], P('grp'), may hold values from -3 to 3
- key_bias: bfloat16 [256], P('grp'), may hold values from -3 to 3
- value_bias: bfloat16 [256], P('grp'), may hold values from -3 to 3
- output_matrix: bfloat16 [768, 1536], P('grp'), may hold values from -0.625 to 0.625
- gate_weight: bfloat16 [4480, 768], P('grp'), may hold values from -0.21875 to 0.21875
- up_weight: bfloat16 [4480, 768], P('grp'), may hold values from -0.21875 to 0.21875
- down_weight: bfloat16 [768, 4480], P('grp'), may hold values from -0.09375 to 0.09375
- attn_gain: bfloat16 [768], P('grp'), may hold values from 0.5 to 1.5
- mlp_gain: bfloat16 [768], P('grp'), may hold values from 0.5 to 1.5
- cotangent: bfloat16 [24576, 768], P(('rep', 'grp')), may hold values from -6 to 6
- seq_lengths: int32 [32, 4], P(('rep', 'grp')), may hold values from 1 to 512, 768 in all within a row
Outputs:
- block_out: float32 [24576, 768], P(('rep', 'grp'))
- input_grad: float32 [24576, 768], P(('rep', 'grp'))
- query_weight_grad: float32 [1536, 768], P('grp')
- key_weight_grad: float32 [256, 768], P('grp')
- value_weight_grad: float32 [256, 768], P('grp')
- query_bias_grad: float32 [1536], P('grp')
- key_bias_grad: float32 [256], P('grp')
- value_bias_grad: float32 [256], P('grp')
- output_weight_grad: float32 [768, 1536], P('grp')
- gate_weight_grad: float32 [4480, 768], P('grp')
- up_weight_grad: float32 [4480, 768], P('grp')
- down_weight_grad: float32 [768, 4480], P('grp')
- attn_gain_grad: float32 [768], P('grp')
- mlp_gain_grad: float32 [768], P('grp')
Inputs may be any that keep to these rules, and one draw needn't show every extreme that they name: `seq_lengths`: each row lists the lengths of the 4 sequences packed on one device; each row sums to 768 and its largest entry is exactly 512.
All inputs are finite; a program needn't handle non-finite values.
Results may differ from a plain program's by a relative error of at most 0.023.
Values may be sent and summed in bfloat16 or wider, within the bound.
A program may use at most 320 MiB of HBM per device.

v0:
```python
import functools
import math

import jax
import jax.numpy as jnp
from jax import lax
from jax.experimental import pallas as pl
from jax.experimental.pallas import tpu as pltpu
from jax.sharding import PartitionSpec as P


HEAD_SIZE = 128

EPSILON = 1e-06
THETA = 1000000.0

BF16 = jnp.bfloat16
F32 = jnp.float32
MESH = pl.DeviceIdType.MESH


def mm_nt(left, right):
    return lax.dot_general(left, right, (((1,), (1,)), ((), ())), preferred_element_type=F32)


def mm_nn(left, right):
    return lax.dot_general(left, right, (((1,), (0,)), ((), ())), preferred_element_type=F32)


def mm_tn(left, right):
    return lax.dot_general(left, right, (((0,), (0,)), ((), ())), preferred_element_type=F32)


def rotary_tables(position, head_dim):
    half_dim = head_dim // 2
    exponent = jnp.arange(half_dim, dtype=F32) * (2.0 / head_dim)
    frequency = jnp.exp(-exponent * math.log(THETA))
    angles = position.astype(F32)[:, None] * frequency[None, :]
    cosine = jnp.cos(angles)
    sine = jnp.sin(angles)
    return (jnp.concatenate([cosine, cosine], axis=-1), jnp.concatenate([sine, sine], axis=-1))


def rms_scale(values):
    return lax.rsqrt(jnp.mean(values * values, axis=-1, keepdims=True) + EPSILON)


def swap(x):
    return lax.ppermute(x, "grp", [(0, 1), (1, 0)])


def after(x, earlier):
    return lax.optimization_barrier((x, earlier))[0]


def swap_shared(x, n_rep, levels=2):
    levels = min(levels, n_rep.bit_length() - 1)
    me = lax.axis_index("rep")
    count = x.shape[0] >> levels
    came = swap(lax.dynamic_slice_in_dim(x, (me & ((1 << levels) - 1)) * count, count, 0))
    for b in range(levels):
        shared = lax.ppermute(came, "rep", [(i, i ^ (1 << b)) for i in range(n_rep)])
        came = in_order(came, shared, (me >> b) & 1)
    return came


def in_order(mine, other, g, axis=0):
    first = jnp.where(g == 0, mine, other)
    second = jnp.where(g == 0, other, mine)
    return jnp.concatenate([first, second], axis)


def half_of(x, which, axis):
    size = x.shape[axis] // 2
    return lax.dynamic_slice_in_dim(x, which * size, size, axis)


def rows_loop(count, step, body):
    def one(i, carry):
        body(pl.multiple_of(i * step, step), step)
        return carry

    lax.fori_loop(0, count // step, one, 0)


def pool_kernel(plan, groups, n_rep, *refs):
    n_parts = sum(len(parts) for _, parts, *_ in groups)
    n_outs = sum(1 if cross else len(cuts) for _, _, _, cuts, cross in groups)
    ins, small_ref, refs = refs[:n_parts], refs[n_parts], refs[n_parts + 1 :]
    outs, small_out, refs = refs[:n_outs], refs[n_outs], refs[n_outs + 1 :]
    pool, full, inbox, flipped, small_box, in_sem, out_sem, send_sem, recv_sem, small_send, small_recv = refs
    me, g = lax.axis_index("rep"), lax.axis_index("grp")
    bits = n_rep.bit_length() - 1
    half = pool.shape[1] // 2

    barrier = pltpu.get_barrier_semaphore()
    for b in range(bits):
        pl.semaphore_signal(barrier, inc=1, device_id={"rep": me ^ (1 << b)}, device_id_type=MESH)
    pl.semaphore_signal(barrier, inc=1, device_id={"grp": 1 - g}, device_id_type=MESH)

    loads, at = [], 0
    for base, parts, end, *_ in groups:
        loads.append([])
        for count in parts:
            loads[-1].append(pltpu.make_async_copy(ins[at], pool.at[pl.ds(base, count)], in_sem.at[at]))
            loads[-1][-1].start()
            base, at = base + count, at + 1
        if base < end:
            pool[pl.ds(base, end - base), :] = jnp.zeros((end - base, pool.shape[1]), BF16)
    small_box[0] = small_ref[...]
    pl.semaphore_wait(barrier, bits + 1)

    copies, state, box_at, used = {}, {}, {}, 0
    for u, (start, size, order, group, cross) in enumerate(plan):
        n = size
        for s in range(bits):
            n //= 2
            box_at[u, s] = used
            used += n
    loaded, numbers, leaving, flips, count_of_flips = set(), {}, [], [], [0]

    def remote(source, target, key, there):
        at = numbers.setdefault(key, len(numbers))
        copies[key] = pltpu.make_async_remote_copy(
            src_ref=source,
            dst_ref=target,
            send_sem=send_sem.at[at],
            recv_sem=recv_sem.at[at],
            device_id=there,
            device_id_type=MESH,
        )
        copies[key].start()

    def bit_of(b):
        return (me >> b) & 1

    def advance(u, step):
        start, size, order, group, cross = plan[u]
        kinds = ["halve"] * bits + ["cross"] * cross + ["double"] * bits + ["out"]
        if step == 0:
            if group not in loaded:
                loaded.add(group)
                for load in loads[group]:
                    load.wait()
            state[u] = [jnp.int32(start), size]
        else:
            copies[u, step - 1].wait()
            before = kinds[step - 1]
            off, n = state[u]
            if before == "halve":
                n //= 2
                at = box_at[u, step - 1]
                keep = pl.multiple_of(off + bit_of(order[step - 1]) * n, n)
                target = full if kinds[step] == "double" else pool

                def add(i, count):
                    there = pl.ds(pl.multiple_of(keep + i, 16), count)
                    here = pl.ds(pl.multiple_of(at + i, 16), count)
                    target[there, :] = (pool[there, :].astype(F32) + inbox[here, :].astype(F32)).astype(BF16)

                rows_loop(n, 16 if n % 32 else 32, add)
                state[u] = [keep, n]
            elif before == "double":
                b = order[2 * bits + cross - step]
                state[u] = [pl.multiple_of(off - bit_of(b) * n, n), 2 * n]
        off, n = state[u]
        kind = kinds[step]
        if kind == "halve":
            n //= 2
            b = order[step]
            give = pl.multiple_of(off + (1 - bit_of(b)) * n, n)
            target = inbox.at[pl.ds(box_at[u, step], n)]
            remote(pool.at[pl.ds(give, n)], target, (u, step), {"rep": me ^ (1 << b)})
        elif kind == "cross":
            rows = pl.ds(off, n)
            mine = pl.ds(pl.multiple_of(g * half, 128), half)
            theirs = pl.ds(pl.multiple_of((1 - g) * half, 128), half)
            remote(pool.at[rows, theirs], full.at[rows, mine], (u, step), {"grp": 1 - g})
            full[rows, mine] = pool[rows, mine]
        elif kind == "double":
            b = order[2 * bits + cross - 1 - step]
            block = pl.ds(off, n)
            remote(full.at[block], full.at[block], (u, step), {"rep": me ^ (1 << b)})
        else:
            first = sum(1 if c else len(cuts) for _, _, _, cuts, c in groups[:group])
            base, _, _, cuts, _ = groups[group]
            wanted = []
            if cross:
                slot = count_of_flips[0] % 2
                if count_of_flips[0] > 1:
                    flips[count_of_flips[0] - 2].wait()
                count_of_flips[0] += 1

                def flip(i, count):
                    piece = full[pl.ds(pl.multiple_of(start + i, 128), count), :].astype(F32)
                    flipped[slot, :, pl.ds(pl.multiple_of(i, 128), count)] = piece.T.astype(BF16)

                rows_loop(size, 128, flip)
                wanted.append((flipped.at[slot, :, pl.ds(0, size)], outs[first].at[:, pl.ds(start - base, size)]))
            for k, count in enumerate(() if cross else cuts):
                low, high = max(base, start), min(base + count, start + size)
                if low < high:
                    wanted.append((full.at[pl.ds(low, high - low)], outs[first + k].at[pl.ds(low - base, high - low)]))
                base += count
            for source, target in wanted:
                copy = pltpu.make_async_copy(source, target, out_sem.at[len(leaving) + len(flips)])
                copy.start()
                (flips if cross else leaving).append(copy)

    def advance_small(s):
        if s > 0:
            copies["small", s - 1].wait()
            if s <= bits:
                small_box[2 * s] = small_box[2 * s - 2] + small_box[2 * s - 1]
        if s <= bits:
            copies["small", s] = pltpu.make_async_remote_copy(
                src_ref=small_box.at[2 * s],
                dst_ref=small_box.at[2 * s + 1],
                send_sem=small_send.at[s],
                recv_sem=small_recv.at[s],
                device_id={"rep": me ^ (1 << s)} if s < bits else {"grp": 1 - g},
                device_id_type=MESH,
            )
            copies["small", s].start()
        else:
            small_out[0] = small_box[2 * bits]
            small_out[1] = small_box[2 * bits + 1]

    steps = [2 * bits + 1 + cross for *_, cross in plan]
    for t in range(max(u + n for u, n in enumerate(steps))):
        for u in range(len(plan)):
            if 0 <= t - u < steps[u]:
                advance(u, t - u)
        if t <= bits + 1:
            advance_small(t)
    for copy in leaving + flips[-2:]:
        copy.wait()


def sum_pool(groups, small, n_rep):
    bits = n_rep.bit_length() - 1
    straight = tuple(range(bits))
    crossed = (0, 2, 1) + tuple(range(3, bits)) if bits >= 3 else straight
    grain = 16 * n_rep
    unit = max(768 // grain, 1) * grain
    flat = [a for arrays, _, _ in groups for a in arrays]
    width = flat[0].shape[1]
    plan, places, outs, base = [], [], [], 0
    for k, (arrays, cuts, cross) in enumerate(groups):
        counts = [a.shape[0] for a in arrays]
        end = base + -(-sum(counts) // grain) * grain
        places.append((base, counts, end, cuts, cross))
        for start in range(base, end, unit):
            order = crossed if len(plan) % 4 == 2 else straight
            plan.append((start, min(unit, end - start), order, k, int(cross)))
        outs += [(width, end - base)] if cross else [(count, width) for count in cuts]
        base = end
    box = sum(size - size // n_rep for _, size, *_ in plan)
    n_copies = sum(2 * bits + cross for *_, cross in plan)
    any_space = pl.BlockSpec(memory_space=pl.ANY)
    vmem = pl.BlockSpec(memory_space=pltpu.VMEM)
    *pieces, sums = pl.pallas_call(
        functools.partial(pool_kernel, plan, places, n_rep),
        out_shape=tuple(jax.ShapeDtypeStruct(shape, BF16) for shape in outs)
        + (jax.ShapeDtypeStruct((2,) + small.shape, F32),),
        in_specs=[any_space] * len(flat) + [vmem],
        out_specs=(any_space,) * len(outs) + (vmem,),
        scratch_shapes=[
            pltpu.VMEM((base, width), BF16),
            pltpu.VMEM((base, width), BF16),
            pltpu.VMEM((box, width), BF16),
            pltpu.VMEM((2, width, unit), BF16),
            pltpu.VMEM((2 * bits + 2,) + small.shape, F32),
            pltpu.SemaphoreType.DMA((len(flat),)),
            pltpu.SemaphoreType.DMA((len(plan) + len(outs),)),
            pltpu.SemaphoreType.DMA((n_copies,)),
            pltpu.SemaphoreType.DMA((n_copies,)),
            pltpu.SemaphoreType.DMA((bits + 1,)),
            pltpu.SemaphoreType.DMA((bits + 1,)),
        ],
        compiler_params=pltpu.CompilerParams(
            collective_id=0, has_side_effects=True, vmem_limit_bytes=60 * 1024 * 1024
        ),
    )(*flat, small)
    return pieces, sums


def ffn_kernel(n2, cot, gate, up, down, hid_out, gg_out, ug_out, ng_out, ngb_out, dp_out, ng_acc, dp_acc):
    step = pl.program_id(0)

    @pl.when(step == 0)
    def _():
        ng_acc[...] = jnp.zeros_like(ng_acc)
        dp_acc[...] = jnp.zeros_like(dp_acc)

    gate_pre = mm_nt(gate[...], n2[...])
    up_proj = mm_nt(up[...], n2[...])
    hidden_grad = mm_nt(down[...], cot[...])
    sigmoid = 1.0 / (1.0 + jnp.exp(-gate_pre))
    activated = gate_pre * sigmoid
    hidden = (activated * up_proj).astype(BF16)
    gate_grad = (hidden_grad * up_proj * sigmoid * (1.0 + gate_pre * (1.0 - sigmoid))).astype(BF16)
    up_grad = (hidden_grad * activated).astype(BF16)
    hid_out[...] = hidden
    gg_out[...] = gate_grad
    ug_out[...] = up_grad
    ng_acc[...] += mm_tn(gate_grad, gate[...]) + mm_tn(up_grad, up[...])
    dp_acc[...] += mm_tn(hidden, down[...])

    @pl.when(step == pl.num_programs(0) - 1)
    def _():
        ng_out[...] = ng_acc[...]
        ngb_out[...] = ng_acc[...].astype(BF16)
        dp_out[...] = dp_acc[...].astype(dp_out.dtype)


def block_of(count, limit, grain):
    return max(d for d in range(grain, limit + 1, grain) if count % d == 0)


def ffn(n2, cot, gate, up, down, part_type):
    rows, width = n2.shape
    units = gate.shape[0]
    block = block_of(units, 512, 16)
    whole = pl.BlockSpec((rows, width), lambda i: (0, 0))
    cut = pl.BlockSpec((block, width), lambda i: (i, 0))
    cut_rows = pl.BlockSpec((block, rows), lambda i: (i, 0))
    wide = jax.ShapeDtypeStruct((units, rows), BF16)
    return pl.pallas_call(
        ffn_kernel,
        grid=(units // block,),
        out_shape=(
            wide,
            wide,
            wide,
            jax.ShapeDtypeStruct((rows, width), F32),
            jax.ShapeDtypeStruct((rows, width), BF16),
            jax.ShapeDtypeStruct((rows, width), part_type),
        ),
        in_specs=[whole, whole, cut, cut, cut],
        out_specs=(cut_rows, cut_rows, cut_rows, whole, whole, whole),
        scratch_shapes=[pltpu.VMEM((rows, width), F32), pltpu.VMEM((rows, width), F32)],
        compiler_params=pltpu.CompilerParams(vmem_limit_bytes=56 * 1024 * 1024),
        cost_estimate=pl.CostEstimate(
            flops=12 * units * rows * width, bytes_accessed=12 * units * width, transcendentals=units * rows
        ),
    )(n2, cot, gate, up, down)


def grads_kernel(hid_a, gg_a, ug_a, hid_b, gg_b, ug_b, n2_a, n2_b, cot_a, cot_b, dw, gw, uw):
    dw[...] = (mm_nn(hid_a[...], cot_a[...]) + mm_nn(hid_b[...], cot_b[...])).astype(BF16)
    gw[...] = (mm_nn(gg_a[...], n2_a[...]) + mm_nn(gg_b[...], n2_b[...])).astype(BF16)
    uw[...] = (mm_nn(ug_a[...], n2_a[...]) + mm_nn(ug_b[...], n2_b[...])).astype(BF16)


def ffn_grads(first, second, n2, cot):
    units, rows = first[0].shape
    width = n2[0].shape[1]
    block = block_of(units, 512, 16)
    whole = pl.BlockSpec((rows, width), lambda i: (0, 0))
    cut = pl.BlockSpec((block, width), lambda i: (i, 0))
    cut_rows = pl.BlockSpec((block, rows), lambda i: (i, 0))
    return pl.pallas_call(
        grads_kernel,
        grid=(units // block,),
        out_shape=(jax.ShapeDtypeStruct((units, width), BF16),) * 3,
        in_specs=[cut_rows] * 6 + [whole] * 4,
        out_specs=(cut,) * 3,
        compiler_params=pltpu.CompilerParams(vmem_limit_bytes=56 * 1024 * 1024),
        cost_estimate=pl.CostEstimate(
            flops=12 * units * rows * width, bytes_accessed=18 * units * width, transcendentals=0
        ),
    )(*first, *second, *n2, *cot)


def turn(x):
    return pltpu.roll(x, HEAD_SIZE // 2, 1)


def head_at(h):
    return pl.ds(pl.multiple_of(h * HEAD_SIZE, HEAD_SIZE), HEAD_SIZE)


def masked_scores(query, key, first, row, count, limit):
    scores = mm_nt(query, key) * (1.0 / math.sqrt(HEAD_SIZE))
    at = lax.broadcasted_iota(jnp.int32, (count, limit), 1)
    line = lax.broadcasted_iota(jnp.int32, (count, limit), 0) + row
    return jnp.where((at <= line) & (at >= first), scores, -1e30)


def front_kernel(
    tokens, gain, qw, kw, vw, qb, kb, vb, cos, sin, first, normed, queries, keys, values, mixed, logs
):
    rows = tokens.shape[0]
    heads = qw.shape[0] // HEAD_SIZE
    block = math.gcd(rows, 256)
    inputs = tokens[...].astype(F32)
    normed[...] = (inputs * rms_scale(inputs) * gain[...]).astype(BF16)
    keys_pre = mm_nt(normed[...], kw[...]) + kb[...]
    keys[...] = (keys_pre * cos[...] + turn(keys_pre) * sin[...]).astype(BF16)
    values[...] = (mm_nt(normed[...], vw[...]) + vb[...]).astype(BF16)
    logs[...] = jnp.zeros_like(logs)
    lane = lax.broadcasted_iota(jnp.int32, (block, HEAD_SIZE), 1)

    def one_head(h, carry):
        lanes = head_at(h)
        pre = mm_nt(normed[...], qw[lanes, :]) + qb[:, lanes]
        queries[:, lanes] = (pre * cos[...] + turn(pre) * sin[...]).astype(BF16)
        for row in range(0, rows, block):
            here, limit = pl.ds(row, block), row + block
            scores = masked_scores(queries[here, lanes], keys[:limit, :], first[here, :], row, block, limit)
            peak = jnp.max(scores, axis=1, keepdims=True)
            weights = jnp.exp(scores - peak)
            sums = jnp.sum(weights, axis=1, keepdims=True)
            logs[here, :] = jnp.where(lane == h, peak + jnp.log(sums), logs[here, :])
            probs = (weights * (1.0 / sums)).astype(BF16)
            mixed[here, lanes] = mm_nn(probs, values[:limit, :]).astype(BF16)
        return carry

    lax.fori_loop(0, heads, one_head, 0)


def front(tokens, gain, weights, biases, tables):
    rows, width = tokens.shape
    features = weights[0].shape[0]
    vmem = pl.BlockSpec(memory_space=pltpu.VMEM)
    return pl.pallas_call(
        front_kernel,
        out_shape=(
            jax.ShapeDtypeStruct((rows, width), BF16),
            jax.ShapeDtypeStruct((rows, features), BF16),
            jax.ShapeDtypeStruct((rows, HEAD_SIZE), BF16),
            jax.ShapeDtypeStruct((rows, HEAD_SIZE), BF16),
            jax.ShapeDtypeStruct((rows, features), BF16),
            jax.ShapeDtypeStruct((rows, HEAD_SIZE), F32),
        ),
        in_specs=[vmem] * 11,
        out_specs=(vmem,) * 6,
        compiler_params=pltpu.CompilerParams(vmem_limit_bytes=48 * 1024 * 1024),
        cost_estimate=pl.CostEstimate(
            flops=40 * rows * features * (width + rows), bytes_accessed=80 * rows * width, transcendentals=0
        ),
    )(tokens, gain, *weights, *biases, *tables)


def project_kernel(mixed, ow, part, part_b):
    part[...] = mm_nt(mixed[...], ow[...])
    part_b[...] = part[...].astype(BF16)


def project(mixed, output_cols):
    shape = mixed.shape[0], output_cols.shape[0]
    vmem = pl.BlockSpec(memory_space=pltpu.VMEM)
    return pl.pallas_call(
        project_kernel,
        out_shape=(jax.ShapeDtypeStruct(shape, F32), jax.ShapeDtypeStruct(shape, BF16)),
        in_specs=[vmem] * 2,
        out_specs=(vmem,) * 2,
        compiler_params=pltpu.CompilerParams(vmem_limit_bytes=16 * 1024 * 1024),
        cost_estimate=pl.CostEstimate(
            flops=2 * mixed.size * shape[1], bytes_accessed=16 * mixed.size, transcendentals=0
        ),
    )(mixed, output_cols)


def back_kernel(
    grad, ow, mixed, queries, keys, values, logs, cos, sin, first, qw, kw, vw, joined, sums, out, out_b, mg, dk, dv
):
    rows, features = queries.shape
    heads = features // HEAD_SIZE
    block = math.gcd(rows, 256)
    scale = 1.0 / math.sqrt(HEAD_SIZE)
    mg[...] = mm_nn(grad[...], ow[...]).astype(BF16)
    dk[...] = jnp.zeros_like(dk)
    dv[...] = jnp.zeros_like(dv)
    lane = lax.broadcasted_iota(jnp.int32, (block, HEAD_SIZE), 1)

    def one_head(h, carry):
        lanes = head_at(h)
        total = jnp.zeros((1, HEAD_SIZE), F32)
        for row in range(0, rows, block):
            here, limit = pl.ds(row, block), row + block
            query, grads = queries[here, lanes], mg[here, lanes]
            scores = masked_scores(query, keys[:limit, :], first[here, :], row, block, limit)
            log_total = jnp.sum(jnp.where(lane == h, logs[here, :], 0.0), axis=1, keepdims=True)
            probs = jnp.exp(scores - log_total)
            delta = jnp.sum(grads.astype(F32) * mixed[here, lanes].astype(F32), axis=1, keepdims=True)
            probs_grad = mm_nt(grads, values[:limit, :])
            score_grad = (probs * (probs_grad - delta) * scale).astype(BF16)
            dv[:limit, :] += mm_tn(probs.astype(BF16), grads)
            dk[:limit, :] += mm_tn(score_grad, query)
            dq = mm_nn(score_grad, keys[:limit, :])
            dq = dq * cos[here, :] - turn(dq) * sin[here, :]
            total = total + jnp.sum(dq, axis=0, keepdims=True)
            joined[here, lanes] = dq.astype(BF16)
        sums[:, lanes] = total
        return carry

    lax.fori_loop(0, heads, one_head, 0)
    keys_grad = dk[...] * cos[...] - turn(dk[...]) * sin[...]
    for k, piece in enumerate((keys_grad, dv[...])):
        lanes = pl.ds(features + k * HEAD_SIZE, HEAD_SIZE)
        sums[:, lanes] = jnp.sum(piece, axis=0, keepdims=True)
        joined[:, lanes] = piece.astype(BF16)
    out[...] = (
        mm_nn(joined[:, :features], qw[...])
        + mm_nn(joined[:, features : features + HEAD_SIZE], kw[...])
        + mm_nn(joined[:, features + HEAD_SIZE :], vw[...])
    )
    out_b[...] = out[...].astype(BF16)


def back(grad, output_cols, kept, tables, weights):
    rows, width = grad.shape
    features = weights[0].shape[0]
    vmem = pl.BlockSpec(memory_space=pltpu.VMEM)
    return pl.pallas_call(
        back_kernel,
        out_shape=(
            jax.ShapeDtypeStruct((rows, features + 2 * HEAD_SIZE), BF16),
            jax.ShapeDtypeStruct((1, features + 2 * HEAD_SIZE), F32),
            jax.ShapeDtypeStruct((rows, width), F32),
            jax.ShapeDtypeStruct((rows, width), BF16),
        ),
        in_specs=[vmem] * 13,
        out_specs=(vmem,) * 4,
        scratch_shapes=[
            pltpu.VMEM((rows, features), BF16),
            pltpu.VMEM((rows, HEAD_SIZE), F32),
            pltpu.VMEM((rows, HEAD_SIZE), F32),
        ],
        compiler_params=pltpu.CompilerParams(vmem_limit_bytes=48 * 1024 * 1024),
        cost_estimate=pl.CostEstimate(
            flops=40 * rows * features * (width + 2 * rows), bytes_accessed=80 * rows * width, transcendentals=0
        ),
    )(grad, output_cols, *kept, *tables, *weights)


def mask_and_tables(lengths, rows):
    ends = jnp.cumsum(lengths)
    starts = ends - lengths
    row = jnp.arange(rows, dtype=jnp.int32)
    inside = (row[:, None] >= starts[None, :]) & (row[:, None] < ends[None, :])
    first = jnp.sum(jnp.where(inside, starts[None, :], 0), axis=1)
    cosine, sine = rotary_tables(row - first, HEAD_SIZE)
    half = HEAD_SIZE // 2
    sine = jnp.concatenate([-sine[:, :half], sine[:, half:]], axis=1)
    return cosine, sine, first[:, None]


def local(
    n_rep,
    tokens,
    query_weight,
    key_weight,
    value_weight,
    query_bias,
    key_bias,
    value_bias,
    output_matrix,
    gate_weight,
    up_weight,
    down_weight,
    attn_gain,
    mlp_gain,
    cotangent,
    seq_lengths,
):
    g = lax.axis_index("grp")
    rows = tokens.shape[0]

    gains = jnp.stack([attn_gain, mlp_gain])
    gains_other = swap(gains)
    tokens_other = swap(tokens)
    lengths_other = swap(seq_lengths)
    cut = output_matrix.shape[1] // 2
    given = jnp.concatenate([half_of(output_matrix, 1 - g, 1), half_of(down_weight, 1 - g, 1)], axis=1)
    shared = swap_shared(given, n_rep)
    gains = in_order(gains, gains_other, g, 1).astype(F32)
    attn_gain_all, mlp_gain_all = gains[0:1], gains[1:2]
    output_cols = in_order(half_of(output_matrix, g, 1), shared[:, :cut], g)
    down_rows = in_order(half_of(down_weight, g, 1), shared[:, cut:], g).T

    weights = (query_weight, key_weight, value_weight)
    biases = tuple(b.astype(F32)[None, :] for b in (query_bias, key_bias, value_bias))

    def begin(token_rows, lengths):
        tables = mask_and_tables(lengths[0], rows)
        normed, queries, keys, values, mixed, logs = front(token_rows, attn_gain_all, weights, biases, tables)
        inputs = token_rows.astype(F32)
        return dict(
            inputs=inputs,
            unit=inputs * rms_scale(inputs),
            scale=rms_scale(inputs),
            normed=normed,
            kept=(mixed, queries, keys, values, logs),
            tables=tables,
        )

    own = begin(tokens, seq_lengths)
    cotangent_other = swap(after(cotangent, own["kept"][0]))
    own["part"], part_own_b = project(own["kept"][0], output_cols)
    came_other = swap(part_own_b)
    oth = begin(after(tokens_other, own["kept"][0]), lengths_other)
    oth["part"], part_oth_b = project(oth["kept"][0], output_cols)
    came_own = swap(after(part_oth_b, part_own_b))

    def middle(kept, came, cot, part_type):
        residual = kept["inputs"] + kept["part"] + came.astype(F32)
        scale = rms_scale(residual)
        normed = (residual * scale * mlp_gain_all).astype(BF16)
        *wide, grad, grad_b, part = ffn(normed, cot, gate_weight, up_weight, down_rows, part_type)
        return dict(residual=residual, scale=scale, normed=normed, wide=wide, grad=grad, grad_b=grad_b, part=part)

    mid_oth = middle(oth, came_other, cotangent_other, BF16)
    grad_came_own = swap(mid_oth["grad_b"])
    mid_own = middle(own, came_own, cotangent, F32)
    grad_came_oth = swap(after(mid_own["grad_b"], grad_came_own))
    down_came = swap(after(mid_oth["part"], grad_came_oth))
    block_out = mid_own["residual"] + mid_own["part"] + down_came.astype(F32)
    down_grad, gate_weight_grad, up_weight_grad = ffn_grads(
        mid_oth["wide"],
        mid_own["wide"],
        (mid_oth["normed"], mid_own["normed"]),
        (cotangent_other, cotangent),
    )

    def middle_grad(mid, came, cot):
        normed_grad = mid["grad"] + came.astype(F32)
        unit = mid["residual"] * mid["scale"]
        gain_grad = jnp.sum(normed_grad * unit, axis=0)
        unit_grad = normed_grad * mlp_gain_all
        residual_grad = cot.astype(F32) + mid["scale"] * (
            unit_grad - unit * jnp.mean(unit_grad * unit, axis=-1, keepdims=True)
        )
        return residual_grad, residual_grad.astype(BF16), gain_grad

    residual_grad_own, residual_grad_own_b, gain_grad_own = middle_grad(mid_own, grad_came_own, cotangent)
    _, residual_grad_oth_b, gain_grad_oth = middle_grad(mid_oth, grad_came_oth, cotangent_other)
    mlp_gain_grad = gain_grad_own + gain_grad_oth

    joined_own, sums_own, front_own, _ = back(residual_grad_own_b, output_cols, own["kept"], own["tables"], weights)
    joined_oth, sums_oth, front_oth, front_oth_b = back(
        residual_grad_oth_b, output_cols, oth["kept"], oth["tables"], weights
    )
    front_came = swap(after(front_oth_b, down_came))
    output_grad = mm_tn(
        jnp.concatenate([own["kept"][0], oth["kept"][0]]), jnp.concatenate([residual_grad_own_b, residual_grad_oth_b])
    ).astype(BF16)
    projections = mm_tn(
        jnp.concatenate([joined_own, joined_oth]), jnp.concatenate([own["normed"], oth["normed"]])
    ).astype(BF16)
    attn_gain_grad = jnp.sum(front_own * own["unit"] + front_oth * oth["unit"], axis=0)
    front_own = front_own + front_came.astype(F32)
    unit_grad = front_own * attn_gain_all
    input_grad = residual_grad_own + own["scale"] * (
        unit_grad - own["unit"] * jnp.mean(unit_grad * own["unit"], axis=-1, keepdims=True)
    )

    small = jnp.concatenate([(sums_own + sums_oth)[0], half_of(mlp_gain_grad, g, 0), attn_gain_grad])
    count = small.shape[0]
    lines = -(-count // (8 * 128)) * 8
    small = jnp.pad(small, (0, lines * 128 - count)).reshape(lines, 128)
    units, features = gate_weight.shape[0], query_weight.shape[0]
    pieces, small = sum_pool(
        [
            ([down_grad], [units], True),
            ([gate_weight_grad, up_weight_grad], [units, units], False),
            ([output_grad], [features], True),
            ([projections], [w.shape[0] for w in weights], False),
        ],
        small,
        n_rep,
    )
    small = small.reshape(2, -1)
    vectors, at = [], 0
    for piece in (query_bias, key_bias, value_bias, mlp_gain):
        vectors.append(small[0, at : at + piece.shape[0]])
        at += piece.shape[0]
    vectors.append(half_of(small[0, at:count] + small[1, at:count], g, 0))
    half = down_grad.shape[1] // 2

    def owned(piece, count):
        return jnp.concatenate([piece[:half, :count], piece[half:, :count]], axis=1).astype(F32)

    return (
        block_out,
        input_grad,
        pieces[4].astype(F32),
        pieces[5].astype(F32),
        pieces[6].astype(F32),
        vectors[0],
        vectors[1],
        vectors[2],
        owned(pieces[3], features),
        pieces[1].astype(F32),
        pieces[2].astype(F32),
        owned(pieces[0], units),
        vectors[4],
        vectors[3],
    )


def solution(mesh):
    n_rep = mesh.shape["rep"]
    assert mesh.shape["grp"] == 2 and n_rep & (n_rep - 1) == 0
    rows = P(("rep", "grp"), None)
    wide, flat = P("grp", None), P("grp")

    def body(*args):
        return local(n_rep, *args)

    return jax.shard_map(
        body,
        mesh=mesh,
        in_specs=(rows, wide, wide, wide, flat, flat, flat, wide, wide, wide, wide, flat, flat, rows, rows),
        out_specs=(rows, rows, wide, wide, wide, flat, flat, flat, wide, wide, wide, wide, flat, flat),
        check_vma=False,
    )
```

profile of v0, /device:TPU:9, one launch (start us, length us, event | category | flops | bytes accessed | tf_op | source)
XLA Modules:
  0.0 477.3 jit_solution(12940485365685491115)
XLA Ops:
  0.7 2.2 constant_dynamic-slice_fusion.2
  10.5 8.9 %collective-permute-done.5 = s32[1,4]{1,0:T(1,128)S(1)} collective-permute-done((s32[1,4]{1,0:T(1,128)}, s32[1,4]{1,0:T(1,128)S(1)}, u32[]{:S(2)}, u32[]{:S(2)}) %collective-permute-start.5) | collective-permute-done | bytes 48 | tf_op jit(solution)/shard_map/ppermute | solution.py:49
  19.7 2.8 fusion.40
  22.8 2.8 collective-permute-start.2
  28.8 17.2 %shard_map.254 = (bf16[768,768]{1,0:T(8,128)(2,1)S(1)}, bf16[768,768]{1,0:T(8,128)(2,1)S(1)}, bf16[768,128]{1,0:T(8,128)(2,1)S(1)}, bf16[768,128]{1,0:T(8,128)(2...) custom-call(bf16[768,768]{1,0:T(8,128)(2,1)} %tokens.1, f32[1,768]{1,0:T(1,128)S(1)} %get-tuple-element.152.gain, ...), custom_call_target="tpu_custom_call" | custom-call | flops 36238786560 | bytes 47185920 | tf_op jit(solution)/shard_map/pallas_call | solution.py:427
  47.4 7.4 %collective-permute-done.3 = bf16[192,3008]{1,0:T(8,128)(2,1)S(1)} collective-permute-done((bf16[192,3008]{1,0:T(8,128)(2,1)S(1)}, bf16[192,3008]{1,0:T(8,128)(2,1)S(1)}, u32[]{:S(2)}, u32[]{:S(2)}) %collective-permute-start.3) | collective-permute-done | bytes 1155104 | tf_op jit(solution)/shard_map/ppermute | solution.py:62
  56.0 2.1 shard_map.255
  59.3 17.0 %shard_map.256 = (bf16[768,768]{1,0:T(8,128)(2,1)S(1)}, bf16[768,768]{1,0:T(8,128)(2,1)S(1)}, bf16[768,128]{1,0:T(8,128)(2,1)S(1)}, bf16[768,128]{1,0:T(8,128)(2...) custom-call(bf16[768,768]{1,0:T(8,128)(2,1)} %copy-done.47, f32[1,768]{1,0:T(1,128)S(1)} %get-tuple-element.152.gain, ...), custom_call_target="tpu_custom_call" | custom-call | flops 36238786560 | bytes 47185920 | tf_op jit(solution)/shard_map/pallas_call | solution.py:427
  81.1 3.1 broadcast_select_fusion.1
  86.3 5.7 %copy.39.down = bf16[2240,768]{1,0:T(8,128)(2,1)} copy(bf16[2240,768]{0,1:T(8,128)(2,1)} %maximum_bitcast_fusion) | data formatting | bytes 6881280 | tf_op jit(solution)/shard_map/transpose | solution.py:582
  92.0 6.6 %collective-permute-done.7 = bf16[768,768]{1,0:T(8,128)(2,1)} collective-permute-done((bf16[768,768]{1,0:T(8,128)(2,1)}, bf16[768,768]{1,0:T(8,128)(2,1)}, u32[]{:S(2)}, u32[]{:S(2)}) %collective-permute-start.7) | collective-permute-done | bytes 1179680 | tf_op jit(solution)/shard_map/ppermute | solution.py:49
  98.6 3.7 multiply_reduce_fusion.4
  102.3 21.6 %collective-permute-done.6 = bf16[768,768]{1,0:T(8,128)(2,1)} collective-permute-done((bf16[768,768]{1,0:T(8,128)(2,1)}, bf16[768,768]{1,0:T(8,128)(2,1)}, u32[]{:S(2)}, u32[]{:S(2)}) %collective-permute-start.6) | collective-permute-done | bytes 1179680 | tf_op jit(solution)/shard_map/ppermute | solution.py:49
  123.9 2.6 multiply_reduce_fusion.5
  128.4 27.7 %shard_map.259 = (bf16[2240,768]{1,0:T(8,128)(2,1)}, bf16[2240,768]{1,0:T(8,128)(2,1)}, bf16[2240,768]{1,0:T(8,128)(2,1)}, f32[768,768]{1,0:T(8,128)}, bf16[768,...) custom-call(bf16[768,768]{1,0:T(8,128)(2,1)} %get-tuple-element.161.n2.n2_a, ...), custom_call_target="tpu_custom_call" | custom-call | flops 15854469120 | bytes 20643840 | tf_op jit(solution)/shard_map/pallas_call | solution.py:329
  158.6 27.9 %shard_map.258 = (bf16[2240,768]{1,0:T(8,128)(2,1)}, bf16[2240,768]{1,0:T(8,128)(2,1)}, bf16[2240,768]{1,0:T(8,128)(2,1)}, f32[768,768]{1,0:T(8,128)}, bf16[768,768]{1,0:T(8,128)(2,1)}, /*index=5*/f32[768,768]{1,0:T(8,128)}) custom-call(bf16[768,768]{1,0:T(8,128)(2,1)} %get-tuple-element.160.n2.n2_b, bf16[768,768]{1,0:T(8,128)(2,1)} %cot_b.1, ...), custom_call_target="tpu_custom_call" | custom-call | flops 15854469120 | bytes 20643840 | tf_op jit(solution)/shard_map/pallas_call | solution.py:329
  187.5 22.0 %shard_map.262 = (bf16[2240,768]{1,0:T(8,128)(2,1)}, bf16[2240,768]{1,0:T(8,128)(2,1)}, bf16[2240,768]{1,0:T(8,128)(2,1)}) custom-call(bf16[2240,768]{1,0:T(8,128)(2,1)} %get-tuple-element.94.hid_a, bf16[2240,768]{1,0:T(8,128)(2,1)} %get-tuple-element.95.gg_a, bf16[2240,768]{1,0:T(8,128)(2,1)} %get-tuple-element.96.ug_a, ...), custom_call_target="tpu_custom_call" | custom-call | flops 15854469120 | bytes 30965760 | tf_op jit(solution)/shard_map/pallas_call | solution.py:363
  209.5 3.1 collective-permute-done.10
  212.6 2.2 multiply_reduce_fusion
  215.1 3.7 multiply_reduce_fusion.1
  218.9 18.1 %shard_map.261 = (bf16[768,1024]{1,0:T(8,128)(2,1)}, f32[1,1024]{1,0:T(1,128)S(1)}, f32[768,768]{1,0:T(8,128)}, bf16[768,768]{1,0:T(8,128)(2,1)S(1)}) custom-call(bf16[768,768]{1,0:T(8,128)(2,1)S(1)} %get-tuple-element.159.grad, bf16[768,768]{1,0:T(8,128)(2,1)S(1)} %pad_maximum_fusion.2.ow, bf16[768,768]{1,0:T(8,128)(2,1)} %copy-done.19, ...), custom_call_target="tpu_custom_call" | custom-call | flops 54358179840 | bytes 47185920 | tf_op jit(solution)/shard_map/pallas_call | solution.py:517
  237.1 3.0 collective-permute-done.11
  240.3 5.7 %fusion.50 = (bf16[768,768]{1,0:T(8,128)(2,1)S(1)}, f32[768,768]{1,0:T(8,128)}, f32[768,768]{1,0:T(8,128)}) fusion(f32[768]{0:T(1024)S(1)} %broadcast_multiply_fusion.2, f32[768,768]{1,0:T(8,128)S(1)} %get-tuple-element.129, f32[768]{0:T(1024)S(1)} %get-tuple-element.125, f32[768,768]{1,0:T(8,128)S(1)} %copy-done.45, bf16[768,768]{1,0:T(8,128)(2,1)S(1)} %copy-done.50, ...), kind=kLoop, calls=%fused_computation.125 | loop fusion | flops 7667712 | bytes 16524288 | tf_op jit(solution)/shard_map/convert_element_type | solution.py:636
  246.0 18.9 %shard_map.260 = (bf16[768,1024]{1,0:T(8,128)(2,1)}, f32[1,1024]{1,0:T(1,128)S(1)}, f32[768,768]{1,0:T(8,128)}, bf16[768,768]{1,0:T(8,128)(2,1)}) custom-call(bf16[768,768]{1,0:T(8,128)(2,1)S(1)} %get-tuple-element.126.grad, bf16[768,768]{1,0:T(8,128)(2,1)S(1)} %pad_maximum_fusion.2.ow, bf16[768,768]{1,0:T(8,128)(2,1)} %copy-done.17, ...), custom_call_target="tpu_custom_call" | custom-call | flops 54358179840 | bytes 47185920 | tf_op jit(solution)/shard_map/pallas_call | solution.py:517
  265.0 3.1 fusion.33.refs_3_
  268.2 3.9 fusion.28.refs_4_
  274.1 177.2 %shard_map.263 = (bf16[768,2304]{1,0:T(8,128)(2,1)}, bf16[2240,768]{1,0:T(8,128)(2,1)}, bf16[2240,768]{1,0:T(8,128)(2,1)}, bf16[768,768]{1,0:T(8,128)(2,1)}, bf1...) custom-call(bf16[2240,768]{1,0:T(8,128)(2,1)} %get-tuple-element.100.refs_0_, ...), custom_call_target="tpu_custom_call" | custom-call | tf_op jit(solution)/shard_map/pallas_call | solution.py:262
  453.7 2.4 fusion.53
  456.8 3.4 convert_element_type.114
  460.2 3.4 convert_element_type.115
  468.6 3.7 maximum_convert_fusion
  474.9 2.2 fusion.10
  (217 shorter events, 40.4 us)
Async XLA Ops:
  5.0 17.8 %collective-permute-start.1 = (bf16[96,3008]{1,0:T(8,128)(2,1)}, bf16[96,3008]{1,0:T(8,128)(2,1)S(1)}, u32[]{:S(2)}, u32[]{:S(2)}) collective-permute-start(bf16[96,3008]{1,0:T(8,128)(2,1)} %fusion.38), channel_id=1, source_target_pairs={{0,1},{1,0},{2,3},{3,2},{4,5},{5,4},{6,7},{7,6},{8,9},{9,8},{10,11... | collective-permute-start | bytes 1732616 | tf_op jit(solution)/shard_map/ppermute | solution.py:49
  6.2 13.2 %collective-permute-start.5 = (s32[1,4]{1,0:T(1,128)}, s32[1,4]{1,0:T(1,128)S(1)}, u32[]{:S(2)}, u32[]{:S(2)}) collective-permute-start(s32[1,4]{1,0:T(1,128)} %param.29), channel_id=1, source_target_pairs={{0,1},{1,0},{2,3},{3,2},{4,5},{5,4},{6,7},{7,6},{8,9},{9,8},{10,11... | collective-permute-start | bytes 56 | tf_op jit(solution)/shard_map/ppermute | solution.py:49
  6.5 19.6 %collective-permute-start = (bf16[2,384]{1,0:T(2,128)(2,1)S(1)}, bf16[2,384]{1,0:T(2,128)(2,1)S(1)}, u32[]{:S(2)}, u32[]{:S(2)}) collective-permute-start(bf16[2,384]{1,0:T(2,128)(2,1)S(1)} %pad_maximum_fusion.8), channel_id=1, source_target_pairs={{0,1},{1,0},{2,3},{3,2},{4,5},{5,4},{6,7},{7,6},{8,9},{9,8},{10,11... | collective-permute-start | bytes 4616 | tf_op jit(solution)/shard_map/ppermute | solution.py:49
  7.8 39.6 %collective-permute-start.4 = (bf16[768,768]{1,0:T(8,128)(2,1)S(1)}, bf16[768,768]{1,0:T(8,128)(2,1)S(1)}, u32[]{:S(2)}, u32[]{:S(2)}) collective-permute-start(bf16[768,768]{1,0:T(8,128)(2,1)S(1)} %copy-done.39), channel_id=1, source_target_pairs={{0,1},{1,0},{2,3},{3,2},{4,5},{5,4},{6,7},{7,6},{8,9},{9,8},{10,11... | collective-permute-start | bytes 3538952 | tf_op jit(solution)/shard_map/ppermute | solution.py:49
  9.8 19.0 %copy-start.1 = (s32[768,1]{1,0:T(8,128)}, s32[768,1]{1,0:T(8,128)S(1)}, u32[]{:S(2)}) copy-start(s32[768,1]{1,0:T(8,128)S(1)} %reduce_sum.130.first) | copy-start | bytes 9220
  22.8 4.4 collective-permute-start.2
  25.9 33.4 %copy-start.9 = (f32[768,128]{1,0:T(8,128)}, f32[768,128]{1,0:T(8,128)S(1)}, u32[]{:S(2)}) copy-start(f32[768,128]{1,0:T(8,128)S(1)} %get-tuple-element.169.cos) | copy-start | bytes 1179652
  25.9 33.4 %copy-start.11 = (f32[768,128]{1,0:T(8,128)}, f32[768,128]{1,0:T(8,128)S(1)}, u32[]{:S(2)}) copy-start(f32[768,128]{1,0:T(8,128)S(1)} %get-tuple-element.170.sin) | copy-start | bytes 1179652
  26.1 33.2 %copy-start.3 = (s32[768,1]{1,0:T(8,128)}, s32[768,1]{1,0:T(8,128)S(1)}, u32[]{:S(2)}) copy-start(s32[768,1]{1,0:T(8,128)S(1)} %reduce_sum.131.first) | copy-start | bytes 9220
  27.4 27.3 %collective-permute-start.3 = (bf16[192,3008]{1,0:T(8,128)(2,1)S(1)}, bf16[192,3008]{1,0:T(8,128)(2,1)S(1)}, u32[]{:S(2)}, u32[]{:S(2)}) collective-permute-start(bf16[192,3008]{1,0:T(8,128)(2,1)S(1)} %pad_maximum_fusion.1), channel_id=1, source_target_pairs={{0,4},{2,6},{4,0},{6,2},{8,12},{10,14},{12,8},{14,10},{16,20},{18,... | collective-permute-start | bytes 3465224 | tf_op jit(solution)/shard_map/ppermute | solution.py:62
  46.0 9.4 %copy-start.21 = (bf16[768,768]{1,0:T(8,128)(2,1)}, bf16[768,768]{1,0:T(8,128)(2,1)S(1)}, u32[]{:S(2)}) copy-start(bf16[768,768]{1,0:T(8,128)(2,1)S(1)} %get-tuple-element.105) | copy-start | bytes 3538948
  46.0 9.4 %copy-start.25 = (bf16[768,768]{1,0:T(8,128)(2,1)}, bf16[768,768]{1,0:T(8,128)(2,1)S(1)}, u32[]{:S(2)}) copy-start(bf16[768,768]{1,0:T(8,128)(2,1)S(1)} %get-tuple-element.82.queries) | copy-start | bytes 3538948
  46.0 9.4 %copy-start.27 = (f32[768,128]{1,0:T(8,128)}, f32[768,128]{1,0:T(8,128)S(1)}, u32[]{:S(2)}) copy-start(f32[768,128]{1,0:T(8,128)S(1)} %get-tuple-element.85.logs) | copy-start | bytes 1179652
  46.0 9.4 %copy-start.31 = (bf16[768,128]{1,0:T(8,128)(2,1)}, bf16[768,128]{1,0:T(8,128)(2,1)S(1)}, u32[]{:S(2)}) copy-start(bf16[768,128]{1,0:T(8,128)(2,1)S(1)} %get-tuple-element.83.keys) | copy-start | bytes 589828
  46.0 9.4 %copy-start.33 = (bf16[768,128]{1,0:T(8,128)(2,1)}, bf16[768,128]{1,0:T(8,128)(2,1)S(1)}, u32[]{:S(2)}) copy-start(bf16[768,128]{1,0:T(8,128)(2,1)S(1)} %get-tuple-element.84.values) | copy-start | bytes 589828
  46.0 9.9 %copy-start.17 = (bf16[768,768]{1,0:T(8,128)(2,1)}, bf16[768,768]{1,0:T(8,128)(2,1)S(1)}, u32[]{:S(2)}) copy-start(bf16[768,768]{1,0:T(8,128)(2,1)S(1)} %get-tuple-element.66.mixed) | copy-start | bytes 3538948
  46.0 9.4 %copy-start.53 = (bf16[384,1536]{1,0:T(8,128)(2,1)S(1)}, bf16[384,1536]{1,0:T(8,128)(2,1)}, u32[]{:S(2)}) copy-start(bf16[384,1536]{1,0:T(8,128)(2,1)} %param.22) | copy-start | bytes 3538948
  46.1 82.3 %collective-permute-start.8 = (bf16[768,768]{1,0:T(8,128)(2,1)}, bf16[768,768]{1,0:T(8,128)(2,1)}, u32[]{:S(2)}, u32[]{:S(2)}) collective-permute-start(bf16[768,768]{1,0:T(8,128)(2,1)} %cot_b.1), channel_id=1, source_target_pairs={{0,1},{1,0},{2,3},{3,2},{4,5},{5,4},{6,7},{7,6},{8,9},{9,8},{10,11... | collective-permute-start | bytes 3538952 | tf_op jit(solution)/shard_map/ppermute | solution.py:49
  58.1 40.5 %collective-permute-start.7 = (bf16[768,768]{1,0:T(8,128)(2,1)}, bf16[768,768]{1,0:T(8,128)(2,1)}, u32[]{:S(2)}, u32[]{:S(2)}) collective-permute-start(bf16[768,768]{1,0:T(8,128)(2,1)} %get-tuple-element.71), channel_id=1, source_target_pairs={{0,1},{1,0},{2,3},{3,2},{4,5},{5,4},{6,7},{7,6},{8,9},{9,8},{10,11... | collective-permute-start | bytes 3538952 | tf_op jit(solution)/shard_map/ppermute | solution.py:49
  80.9 43.0 %collective-permute-start.6 = (bf16[768,768]{1,0:T(8,128)(2,1)}, bf16[768,768]{1,0:T(8,128)(2,1)}, u32[]{:S(2)}, u32[]{:S(2)}) collective-permute-start(bf16[768,768]{1,0:T(8,128)(2,1)} %get-tuple-element.72), channel_id=1, source_target_pairs={{0,1},{1,0},{2,3},{3,2},{4,5},{5,4},{6,7},{7,6},{8,9},{9,8},{10,11... | collective-permute-start | bytes 3538952 | tf_op jit(solution)/shard_map/ppermute | solution.py:49
  98.6 25.3 %copy-start.40 = (bf16[768,768]{1,0:T(8,128)(2,1)S(1)}, bf16[768,768]{1,0:T(8,128)(2,1)}, u32[]{:S(2)}) copy-start(bf16[768,768]{1,0:T(8,128)(2,1)} %tokens.1) | copy-start | bytes 3538948
  102.3 24.2 %copy-start.59 = (f32[768]{0:T(1024)}, f32[768]{0:T(1024)S(1)}, u32[]{:S(2)}) copy-start(f32[768]{0:T(1024)S(1)} %add_rsqrt_fusion.2) | copy-start | bytes 9220
  128.4 29.0 %copy-start.64 = (f32[768]{0:T(1024)S(1)}, f32[768]{0:T(1024)}, u32[]{:S(2)}) copy-start(f32[768]{0:T(1024)} %get-tuple-element.144) | copy-start | bytes 9220
  128.4 29.6 %copy-start.65 = (f32[768]{0:T(1024)S(1)}, f32[768]{0:T(1024)}, u32[]{:S(2)}) copy-start(f32[768]{0:T(1024)} %get-tuple-element.143) | copy-start | bytes 9220
  156.1 30.4 %collective-permute-start.9 = (bf16[768,768]{1,0:T(8,128)(2,1)}, bf16[768,768]{1,0:T(8,128)(2,1)S(1)}, u32[]{:S(2)}, u32[]{:S(2)}) collective-permute-start(bf16[768,768]{1,0:T(8,128)(2,1)} %get-tuple-element.78), channel_id=1, source_target_pairs={{0,1},{1,0},{2,3},{3,2},{4,5},{5,4},{6,7},{7,6},{8,9},{9,8},{10,11... | collective-permute-start | bytes 3538952 | tf_op jit(solution)/shard_map/ppermute | solution.py:49
  186.5 26.1 %collective-permute-start.10 = (bf16[768,768]{1,0:T(8,128)(2,1)}, bf16[768,768]{1,0:T(8,128)(2,1)}, u32[]{:S(2)}, u32[]{:S(2)}) collective-permute-start(bf16[768,768]{1,0:T(8,128)(2,1)} %get-tuple-element.79), channel_id=1, source_target_pairs={{0,1},{1,0},{2,3},{3,2},{4,5},{5,4},{6,7},{7,6},{8,9},{9,8},{10,11... | collective-permute-start | bytes 3538952 | tf_op jit(solution)/shard_map/ppermute | solution.py:49
  187.5 25.1 %copy-start.46 = (f32[768,768]{1,0:T(8,128)S(1)}, f32[768,768]{1,0:T(8,128)}, u32[]{:S(2)}) copy-start(f32[768,768]{1,0:T(8,128)} %get-tuple-element.87) | copy-start | bytes 7077892
  187.5 25.1 %copy-start.60 = (f32[768]{0:T(1024)S(1)}, f32[768]{0:T(1024)}, u32[]{:S(2)}) copy-start(f32[768]{0:T(1024)} %copy-done.59) | copy-start | bytes 9220
  214.8 25.3 %collective-permute-start.11 = (bf16[768,768]{1,0:T(8,128)(2,1)}, bf16[768,768]{1,0:T(8,128)(2,1)}, u32[]{:S(2)}, u32[]{:S(2)}) collective-permute-start(bf16[768,768]{1,0:T(8,128)(2,1)} %get-tuple-element.80), channel_id=1, source_target_pairs={{0,1},{1,0},{2,3},{3,2},{4,5},{5,4},{6,7},{7,6},{8,9},{9,8},{10,11... | collective-permute-start | bytes 3538952 | tf_op jit(solution)/shard_map/ppermute | solution.py:49
  240.1 32.0 %collective-permute-start.12 = (bf16[768,768]{1,0:T(8,128)(2,1)S(1)}, bf16[768,768]{1,0:T(8,128)(2,1)S(1)}, u32[]{:S(2)}, u32[]{:S(2)}) collective-permute-start(bf16[768,768]{1,0:T(8,128)(2,1)S(1)} %get-tuple-element.93), channel_id=1, source_target_pairs={{0,1},{1,0},{2,3},{3,2},{4,5},{5,4},{6,7},{7,6},{8,9},{9,8},{10,11... | collective-permute-start | bytes 3538952 | tf_op jit(solution)/shard_map/ppermute | solution.py:49
  246.0 18.9 %copy-start.18 = (bf16[768,768]{1,0:T(8,128)(2,1)S(1)}, bf16[768,768]{1,0:T(8,128)(2,1)}, u32[]{:S(2)}) copy-start(bf16[768,768]{1,0:T(8,128)(2,1)} %copy-done.17) | copy-start | bytes 3538948
  246.0 18.9 %copy-start.20 = (bf16[768,768]{1,0:T(8,128)(2,1)S(1)}, bf16[768,768]{1,0:T(8,128)(2,1)}, u32[]{:S(2)}) copy-start(bf16[768,768]{1,0:T(8,128)(2,1)} %copy-done.19) | copy-start | bytes 3538948
  (53 other events, 223.3 us)
where the time goes:
time: 483 us; the launch traced here: 477 us
  Pallas kernels  330 us (68%)
  other arithmetic  54.4 us (11%)
  waiting for transfers between devices  50.9 us (11%)
  local copies, waits for them, and re-layouts  21.2 us (4%)
  starting transfers between devices  11.9 us (2%)
  matrix products  6.96 us (1%)
    pallas_call x1, Pallas kernels, sum_pool(): pl.pallas_call(functools.partial(pool_kernel, plan, places, n_rep), out_s...  177 us
    pallas_call x2, Pallas kernels, ffn(): pl.pallas_call(ffn_kernel, grid=(units // block,), out_shape=(wide, wide,...  55.5 us
    ppermute x11, waiting for transfers between devices, swap(): return lax.ppermute(x, 'grp', [(0, 1), (1, 0)])  43.1 us
    pallas_call x2, Pallas kernels, back(): pl.pallas_call(back_kernel, out_shape=(jax.ShapeDtypeStruct((rows, featur...  37 us
    pallas_call x2, Pallas kernels, front(): pl.pallas_call(front_kernel, out_shape=(jax.ShapeDtypeStruct((rows, width...  34.2 us
    pallas_call x1, Pallas kernels, ffn_grads(): pl.pallas_call(grads_kernel, grid=(units // block,), out_shape=(jax.Shape...  22 us
  transfers between devices with their start and end apart: 13, of which 7 were waited for; matrix products, arithmetic and copies ran while one was open for 9% of the time, Pallas kernels for 26%

commit v1 on v0

--- a/solution.py
+++ b/solution.py
@@ -57,11 +57,11 @@
     levels = min(levels, n_rep.bit_length() - 1)
     me = lax.axis_index("rep")
     count = x.shape[0] >> levels
-    came = swap(lax.dynamic_slice_in_dim(x, (me & ((1 << levels) - 1)) * count, count, 0))
+    came = piece = swap(lax.dynamic_slice_in_dim(x, (me & ((1 << levels) - 1)) * count, count, 0))
     for b in range(levels):
         shared = lax.ppermute(came, "rep", [(i, i ^ (1 << b)) for i in range(n_rep)])
         came = in_order(came, shared, (me >> b) & 1)
-    return came
+    return came, piece
 
 
 def in_order(mine, other, g, axis=0):
@@ -83,12 +83,14 @@
     lax.fori_loop(0, count // step, one, 0)
 
 
-def pool_kernel(plan, groups, n_rep, *refs):
-    n_parts = sum(len(parts) for _, parts, *_ in groups)
-    n_outs = sum(1 if cross else len(cuts) for _, _, _, cuts, cross in groups)
-    ins, small_ref, refs = refs[:n_parts], refs[n_parts], refs[n_parts + 1 :]
+def pool_kernel(plan, groups, n_factors, slots, n_rep, *refs):
+    n_parts = sum(2 if made else len(parts) for _, parts, _, _, _, made in groups)
+    n_outs = sum(1 if cross else len(cuts) for _, _, _, cuts, cross, _ in groups)
+    ins, factors, refs = refs[:n_parts], refs[n_parts : n_parts + n_factors], refs[n_parts + n_factors :]
+    small_ref, refs = refs[0], refs[1:]
     outs, small_out, refs = refs[:n_outs], refs[n_outs], refs[n_outs + 1 :]
-    pool, full, inbox, flipped, small_box, in_sem, out_sem, send_sem, recv_sem, small_send, small_recv = refs
+    pool, full, inbox, flipped, lefts, small_box, in_sem, left_sem, out_sem, *refs = refs
+    send_sem, recv_sem, small_send, small_recv = refs
     me, g = lax.axis_index("rep"), lax.axis_index("grp")
     bits = n_rep.bit_length() - 1
     half = pool.shape[1] // 2
@@ -99,14 +101,49 @@
     pl.semaphore_signal(barrier, inc=1, device_id={"grp": 1 - g}, device_id_type=MESH)
 
     loads, at = [], 0
-    for base, parts, end, *_ in groups:
+    makers = {}
+    for k, (base, parts, end, _, _, made) in enumerate(groups):
         loads.append([])
-        for count in parts:
-            loads[-1].append(pltpu.make_async_copy(ins[at], pool.at[pl.ds(base, count)], in_sem.at[at]))
-            loads[-1][-1].start()
-            base, at = base + count, at + 1
+        if made:
+            makers[k] = ins[at : at + 2], [factors[f] for f in made]
+            at, base = at + 2, base + parts[0]
+        else:
+            for count in parts:
+                loads[-1].append(pltpu.make_async_copy(ins[at], pool.at[pl.ds(base, count)], in_sem.at[at]))
+                loads[-1][-1].start()
+                base, at = base + count, at + 1
         if base < end:
             pool[pl.ds(base, end - base), :] = jnp.zeros((end - base, pool.shape[1]), BF16)
+    made_units = [u for u, unit in enumerate(plan) if unit[3] in makers]
+    fetched = {}
+
+    def fetch(k):
+        if k < len(made_units):
+            u = made_units[k]
+            start, size, _, group, _ = plan[u]
+            base, parts = groups[group][:2]
+            count = min(size, base + parts[0] - start)
+            fetched[u] = count, []
+            for side, source in enumerate(makers[group][0]):
+                copy = pltpu.make_async_copy(
+                    source.at[pl.ds(start - base, count)], lefts.at[k % slots, side, pl.ds(0, count)], left_sem.at[k, side]
+                )
+                copy.start()
+                fetched[u][1].append(copy)
+
+    def make(u):
+        k = made_units.index(u)
+        start, _, _, group, _ = plan[u]
+        count, waits = fetched[u]
+        for copy in waits:
+            copy.wait()
+        first, second = makers[group][1]
+        product = mm_nn(lefts[k % slots, 0, :count, :], first[...]) + mm_nn(lefts[k % slots, 1, :count, :], second[...])
+        pool[pl.ds(start, count), :] = product.astype(BF16)
+        fetch(k + slots)
+
+    for k in range(slots):
+        fetch(k)
     small_box[0] = small_ref[...]
     pl.semaphore_wait(barrier, bits + 1)
 
@@ -142,6 +179,8 @@
                 loaded.add(group)
                 for load in loads[group]:
                     load.wait()
+            if group in makers:
+                make(u)
             state[u] = [jnp.int32(start), size]
         else:
             copies[u, step - 1].wait()
@@ -182,13 +221,13 @@
             block = pl.ds(off, n)
             remote(full.at[block], full.at[block], (u, step), {"rep": me ^ (1 << b)})
         else:
-            first = sum(1 if c else len(cuts) for _, _, _, cuts, c in groups[:group])
-            base, _, _, cuts, _ = groups[group]
+            first = sum(1 if c else len(cuts) for _, _, _, cuts, c, _ in groups[:group])
+            base, cuts = groups[group][0], groups[group][3]
             wanted = []
             if cross:
-                slot = count_of_flips[0] % 2
-                if count_of_flips[0] > 1:
-                    flips[count_of_flips[0] - 2].wait()
+                slot = count_of_flips[0] % slots
+                if count_of_flips[0] >= slots:
+                    flips[count_of_flips[0] - slots].wait()
                 count_of_flips[0] += 1
 
                 def flip(i, count):
@@ -233,26 +272,25 @@
                 advance(u, t - u)
         if t <= bits + 1:
             advance_small(t)
-    for copy in leaving + flips[-2:]:
+    for copy in leaving + flips[-slots:]:
         copy.wait()
 
 
-def sum_pool(groups, small, n_rep):
+def sum_pool(groups, factors, small, n_rep):
     bits = n_rep.bit_length() - 1
     straight = tuple(range(bits))
-    crossed = (0, 2, 1) + tuple(range(3, bits)) if bits >= 3 else straight
     grain = 16 * n_rep
     unit = max(768 // grain, 1) * grain
-    flat = [a for arrays, _, _ in groups for a in arrays]
-    width = flat[0].shape[1]
+    flat = [a for arrays, *_ in groups for a in arrays]
+    width = factors[0].shape[1]
+    slots = 2 if n_rep <= 16 else 1
     plan, places, outs, base = [], [], [], 0
-    for k, (arrays, cuts, cross) in enumerate(groups):
-        counts = [a.shape[0] for a in arrays]
+    for k, (arrays, cuts, cross, made) in enumerate(groups):
+        counts = [a.shape[0] for a in arrays[: 1 if made else None]]
         end = base + -(-sum(counts) // grain) * grain
-        places.append((base, counts, end, cuts, cross))
+        places.append((base, counts, end, cuts, cross, made))
         for start in range(base, end, unit):
-            order = crossed if len(plan) % 4 == 2 else straight
-            plan.append((start, min(unit, end - start), order, k, int(cross)))
+            plan.append((start, min(unit, end - start), straight, k, int(cross)))
         outs += [(width, end - base)] if cross else [(count, width) for count in cuts]
         base = end
     box = sum(size - size // n_rep for _, size, *_ in plan)
@@ -260,18 +298,20 @@
     any_space = pl.BlockSpec(memory_space=pl.ANY)
     vmem = pl.BlockSpec(memory_space=pltpu.VMEM)
     *pieces, sums = pl.pallas_call(
-        functools.partial(pool_kernel, plan, places, n_rep),
+        functools.partial(pool_kernel, plan, places, len(factors), slots, n_rep),
         out_shape=tuple(jax.ShapeDtypeStruct(shape, BF16) for shape in outs)
         + (jax.ShapeDtypeStruct((2,) + small.shape, F32),),
-        in_specs=[any_space] * len(flat) + [vmem],
+        in_specs=[any_space] * len(flat) + [vmem] * (len(factors) + 1),
         out_specs=(any_space,) * len(outs) + (vmem,),
         scratch_shapes=[
             pltpu.VMEM((base, width), BF16),
             pltpu.VMEM((base, width), BF16),
             pltpu.VMEM((box, width), BF16),
-            pltpu.VMEM((2, width, unit), BF16),
+            pltpu.VMEM((slots, width, unit), BF16),
+            pltpu.VMEM((slots, 2, unit, factors[0].shape[0]), BF16),
             pltpu.VMEM((2 * bits + 2,) + small.shape, F32),
             pltpu.SemaphoreType.DMA((len(flat),)),
+            pltpu.SemaphoreType.DMA((len(plan), 2)),
             pltpu.SemaphoreType.DMA((len(plan) + len(outs),)),
             pltpu.SemaphoreType.DMA((n_copies,)),
             pltpu.SemaphoreType.DMA((n_copies,)),
@@ -279,17 +319,22 @@
             pltpu.SemaphoreType.DMA((bits + 1,)),
         ],
         compiler_params=pltpu.CompilerParams(
-            collective_id=0, has_side_effects=True, vmem_limit_bytes=60 * 1024 * 1024
+            collective_id=0, has_side_effects=True, vmem_limit_bytes=62 * 1024 * 1024
         ),
-    )(*flat, small)
+    )(*flat, *factors, small)
     return pieces, sums
 
 
-def ffn_kernel(n2, cot, gate, up, down, hid_out, gg_out, ug_out, ng_out, ngb_out, dp_out, ng_acc, dp_acc):
+def ffn_kernel(
+    tokens, part, came, gain, cot, gate, up, down, residual, n2, hid_out, gg_out, ug_out, ng_out, ngb_out, dp_out, ng_acc, dp_acc
+):
     step = pl.program_id(0)
 
     @pl.when(step == 0)
     def _():
+        total = tokens[...].astype(F32) + part[...] + came[...].astype(F32)
+        residual[...] = total
+        n2[...] = (total * rms_scale(total) * gain[...]).astype(BF16)
         ng_acc[...] = jnp.zeros_like(ng_acc)
         dp_acc[...] = jnp.zeros_like(dp_acc)
 
@@ -318,8 +363,8 @@
     return max(d for d in range(grain, limit + 1, grain) if count % d == 0)
 
 
-def ffn(n2, cot, gate, up, down, part_type):
-    rows, width = n2.shape
+def ffn(tokens, part, came, gain, cot, gate, up, down, part_type):
+    rows, width = tokens.shape
     units = gate.shape[0]
     block = block_of(units, 512, 16)
     whole = pl.BlockSpec((rows, width), lambda i: (0, 0))
@@ -330,6 +375,8 @@
         ffn_kernel,
         grid=(units // block,),
         out_shape=(
+            jax.ShapeDtypeStruct((rows, width), F32),
+            jax.ShapeDtypeStruct((rows, width), BF16),
             wide,
             wide,
             wide,
@@ -337,40 +384,14 @@
             jax.ShapeDtypeStruct((rows, width), BF16),
             jax.ShapeDtypeStruct((rows, width), part_type),
         ),
-        in_specs=[whole, whole, cut, cut, cut],
-        out_specs=(cut_rows, cut_rows, cut_rows, whole, whole, whole),
+        in_specs=[whole, whole, whole, pl.BlockSpec((1, width), lambda i: (0, 0)), whole, cut, cut, cut],
+        out_specs=(whole, whole, cut_rows, cut_rows, cut_rows, whole, whole, whole),
         scratch_shapes=[pltpu.VMEM((rows, width), F32), pltpu.VMEM((rows, width), F32)],
         compiler_params=pltpu.CompilerParams(vmem_limit_bytes=56 * 1024 * 1024),
         cost_estimate=pl.CostEstimate(
             flops=12 * units * rows * width, bytes_accessed=12 * units * width, transcendentals=units * rows
         ),
-    )(n2, cot, gate, up, down)
-
-
-def grads_kernel(hid_a, gg_a, ug_a, hid_b, gg_b, ug_b, n2_a, n2_b, cot_a, cot_b, dw, gw, uw):
-    dw[...] = (mm_nn(hid_a[...], cot_a[...]) + mm_nn(hid_b[...], cot_b[...])).astype(BF16)
-    gw[...] = (mm_nn(gg_a[...], n2_a[...]) + mm_nn(gg_b[...], n2_b[...])).astype(BF16)
-    uw[...] = (mm_nn(ug_a[...], n2_a[...]) + mm_nn(ug_b[...], n2_b[...])).astype(BF16)
-
-
-def ffn_grads(first, second, n2, cot):
-    units, rows = first[0].shape
-    width = n2[0].shape[1]
-    block = block_of(units, 512, 16)
-    whole = pl.BlockSpec((rows, width), lambda i: (0, 0))
-    cut = pl.BlockSpec((block, width), lambda i: (i, 0))
-    cut_rows = pl.BlockSpec((block, rows), lambda i: (i, 0))
-    return pl.pallas_call(
-        grads_kernel,
-        grid=(units // block,),
-        out_shape=(jax.ShapeDtypeStruct((units, width), BF16),) * 3,
-        in_specs=[cut_rows] * 6 + [whole] * 4,
-        out_specs=(cut,) * 3,
-        compiler_params=pltpu.CompilerParams(vmem_limit_bytes=56 * 1024 * 1024),
-        cost_estimate=pl.CostEstimate(
-            flops=12 * units * rows * width, bytes_accessed=18 * units * width, transcendentals=0
-        ),
-    )(*first, *second, *n2, *cot)
+    )(tokens, part, came, gain, cot, gate, up, down)
 
 
 def turn(x):
@@ -464,13 +485,22 @@
 
 
 def back_kernel(
-    grad, ow, mixed, queries, keys, values, logs, cos, sin, first, qw, kw, vw, joined, sums, out, out_b, mg, dk, dv
+    tokens, grad, came, residual, cot, gain, ow, mixed, queries, keys, values, logs, cos, sin, first, qw, kw, vw,
+    residual_grad, residual_grad_b, gain_grad, front_gain_grad, joined, sums, out, out_b, mg, dk, dv
 ):
     rows, features = queries.shape
     heads = features // HEAD_SIZE
     block = math.gcd(rows, 256)
     scale = 1.0 / math.sqrt(HEAD_SIZE)
-    mg[...] = mm_nn(grad[...], ow[...]).astype(BF16)
+    normed_grad = grad[...] + came[...].astype(F32)
+    norm = rms_scale(residual[...])
+    unit = residual[...] * norm
+    gain_grad[...] = jnp.sum(normed_grad * unit, axis=0, keepdims=True)
+    unit_grad = normed_grad * gain[...]
+    along = jnp.mean(unit_grad * unit, axis=1, keepdims=True)
+    residual_grad[...] = cot[...].astype(F32) + norm * (unit_grad - unit * along)
+    residual_grad_b[...] = residual_grad[...].astype(BF16)
+    mg[...] = mm_nn(residual_grad_b[...], ow[...]).astype(BF16)
     dk[...] = jnp.zeros_like(dk)
     dv[...] = jnp.zeros_like(dv)
     lane = lax.broadcasted_iota(jnp.int32, (block, HEAD_SIZE), 1)
@@ -508,22 +538,28 @@
         + mm_nn(joined[:, features + HEAD_SIZE :], vw[...])
     )
     out_b[...] = out[...].astype(BF16)
-
-
-def back(grad, output_cols, kept, tables, weights):
+    inputs = tokens[...].astype(F32)
+    front_gain_grad[...] = jnp.sum(out[...] * (inputs * rms_scale(inputs)), axis=0, keepdims=True)
+
+
+def back(tokens, grad, came, residual, cot, gain, output_cols, kept, tables, weights):
     rows, width = grad.shape
     features = weights[0].shape[0]
     vmem = pl.BlockSpec(memory_space=pltpu.VMEM)
     return pl.pallas_call(
         back_kernel,
         out_shape=(
+            jax.ShapeDtypeStruct((rows, width), F32),
+            jax.ShapeDtypeStruct((rows, width), BF16),
+            jax.ShapeDtypeStruct((1, width), F32),
+            jax.ShapeDtypeStruct((1, width), F32),
             jax.ShapeDtypeStruct((rows, features + 2 * HEAD_SIZE), BF16),
             jax.ShapeDtypeStruct((1, features + 2 * HEAD_SIZE), F32),
             jax.ShapeDtypeStruct((rows, width), F32),
             jax.ShapeDtypeStruct((rows, width), BF16),
         ),
-        in_specs=[vmem] * 13,
-        out_specs=(vmem,) * 4,
+        in_specs=[vmem] * 18,
+        out_specs=(vmem,) * 8,
         scratch_shapes=[
             pltpu.VMEM((rows, features), BF16),
             pltpu.VMEM((rows, HEAD_SIZE), F32),
@@ -533,7 +569,7 @@
         cost_estimate=pl.CostEstimate(
             flops=40 * rows * features * (width + 2 * rows), bytes_accessed=80 * rows * width, transcendentals=0
         ),
-    )(grad, output_cols, *kept, *tables, *weights)
+    )(tokens, grad, came, residual, cot, gain, output_cols, *kept, *tables, *weights)
 
 
 def mask_and_tables(lengths, rows):
@@ -571,11 +607,11 @@
 
     gains = jnp.stack([attn_gain, mlp_gain])
     gains_other = swap(gains)
-    tokens_other = swap(tokens)
     lengths_other = swap(seq_lengths)
     cut = output_matrix.shape[1] // 2
     given = jnp.concatenate([half_of(output_matrix, 1 - g, 1), half_of(down_weight, 1 - g, 1)], axis=1)
-    shared = swap_shared(given, n_rep)
+    shared, came = swap_shared(given, n_rep)
+    tokens_other = swap(after(tokens, came))
     gains = in_order(gains, gains_other, g, 1).astype(F32)
     attn_gain_all, mlp_gain_all = gains[0:1], gains[1:2]
     output_cols = in_order(half_of(output_matrix, g, 1), shared[:, :cut], g)
@@ -589,7 +625,7 @@
         normed, queries, keys, values, mixed, logs = front(token_rows, attn_gain_all, weights, biases, tables)
         inputs = token_rows.astype(F32)
         return dict(
-            inputs=inputs,
+            tokens=token_rows,
             unit=inputs * rms_scale(inputs),
             scale=rms_scale(inputs),
             normed=normed,
@@ -601,16 +637,15 @@
     cotangent_other = swap(after(cotangent, own["kept"][0]))
     own["part"], part_own_b = project(own["kept"][0], output_cols)
     came_other = swap(part_own_b)
-    oth = begin(after(tokens_other, own["kept"][0]), lengths_other)
+    oth = begin(after(tokens_other, own["kept"][0]), after(lengths_other, own["kept"][0]))
     oth["part"], part_oth_b = project(oth["kept"][0], output_cols)
     came_own = swap(after(part_oth_b, part_own_b))
 
     def middle(kept, came, cot, part_type):
-        residual = kept["inputs"] + kept["part"] + came.astype(F32)
-        scale = rms_scale(residual)
-        normed = (residual * scale * mlp_gain_all).astype(BF16)
-        *wide, grad, grad_b, part = ffn(normed, cot, gate_weight, up_weight, down_rows, part_type)
-        return dict(residual=residual, scale=scale, normed=normed, wide=wide, grad=grad, grad_b=grad_b, part=part)
+        residual, normed, *wide, grad, grad_b, part = ffn(
+            kept["tokens"], kept["part"], came, mlp_gain_all, cot, gate_weight, up_weight, down_rows, part_type
+        )
+        return dict(residual=residual, normed=normed, wide=wide, grad=grad, grad_b=grad_b, part=part)
 
     mid_oth = middle(oth, came_other, cotangent_other, BF16)
     grad_came_own = swap(mid_oth["grad_b"])
@@ -618,39 +653,27 @@
     grad_came_oth = swap(after(mid_own["grad_b"], grad_came_own))
     down_came = swap(after(mid_oth["part"], grad_came_oth))
     block_out = mid_own["residual"] + mid_own["part"] + down_came.astype(F32)
-    down_grad, gate_weight_grad, up_weight_grad = ffn_grads(
-        mid_oth["wide"],
-        mid_own["wide"],
-        (mid_oth["normed"], mid_own["normed"]),
-        (cotangent_other, cotangent),
+
+    def end(mid, came, cot, kept):
+        return back(
+            kept["tokens"], mid["grad"], came, mid["residual"], cot, mlp_gain_all, output_cols, kept["kept"], kept["tables"], weights
+        )
+
+    residual_grad_own, residual_grad_own_b, gain_grad_own, front_gain_own, joined_own, sums_own, front_own, _ = end(
+        mid_own, grad_came_own, cotangent, own
     )
-
-    def middle_grad(mid, came, cot):
-        normed_grad = mid["grad"] + came.astype(F32)
-        unit = mid["residual"] * mid["scale"]
-        gain_grad = jnp.sum(normed_grad * unit, axis=0)
-        unit_grad = normed_grad * mlp_gain_all
-        residual_grad = cot.astype(F32) + mid["scale"] * (
-            unit_grad - unit * jnp.mean(unit_grad * unit, axis=-1, keepdims=True)
-        )
-        return residual_grad, residual_grad.astype(BF16), gain_grad
-
-    residual_grad_own, residual_grad_own_b, gain_grad_own = middle_grad(mid_own, grad_came_own, cotangent)
-    _, residual_grad_oth_b, gain_grad_oth = middle_grad(mid_oth, grad_came_oth, cotangent_other)
-    mlp_gain_grad = gain_grad_own + gain_grad_oth
-
-    joined_own, sums_own, front_own, _ = back(residual_grad_own_b, output_cols, own["kept"], own["tables"], weights)
-    joined_oth, sums_oth, front_oth, front_oth_b = back(
-        residual_grad_oth_b, output_cols, oth["kept"], oth["tables"], weights
+    _, residual_grad_oth_b, gain_grad_oth, front_gain_oth, joined_oth, sums_oth, _, front_oth_b = end(
+        mid_oth, grad_came_oth, cotangent_other, oth
     )
-    front_came = swap(after(front_oth_b, down_came))
+    mlp_gain_grad = (gain_grad_own + gain_grad_oth)[0]
+    front_came = swap(front_oth_b)
     output_grad = mm_tn(
         jnp.concatenate([own["kept"][0], oth["kept"][0]]), jnp.concatenate([residual_grad_own_b, residual_grad_oth_b])
     ).astype(BF16)
     projections = mm_tn(
         jnp.concatenate([joined_own, joined_oth]), jnp.concatenate([own["normed"], oth["normed"]])
     ).astype(BF16)
-    attn_gain_grad = jnp.sum(front_own * own["unit"] + front_oth * oth["unit"], axis=0)
+    attn_gain_grad = (front_gain_own + front_gain_oth)[0]
     front_own = front_own + front_came.astype(F32)
     unit_grad = front_own * attn_gain_all
     input_grad = residual_grad_own + own["scale"] * (
@@ -664,11 +687,13 @@
     units, features = gate_weight.shape[0], query_weight.shape[0]
     pieces, small = sum_pool(
         [
-            ([down_grad], [units], True),
-            ([gate_weight_grad, up_weight_grad], [units, units], False),
-            ([output_grad], [features], True),
-            ([projections], [w.shape[0] for w in weights], False),
+            ([mid_oth["wide"][0], mid_own["wide"][0]], [units], True, (0, 1)),
+            ([mid_oth["wide"][1], mid_own["wide"][1]], [units], False, (2, 3)),
+            ([mid_oth["wide"][2], mid_own["wide"][2]], [units], False, (2, 3)),
+            ([output_grad], [features], True, None),
+            ([projections], [w.shape[0] for w in weights], False, None),
         ],
+        [cotangent_other, cotangent, mid_oth["normed"], mid_own["normed"]],
         small,
         n_rep,
     )
@@ -678,7 +703,7 @@
         vectors.append(small[0, at : at + piece.shape[0]])
         at += piece.shape[0]
     vectors.append(half_of(small[0, at:count] + small[1, at:count], g, 0))
-    half = down_grad.shape[1] // 2
+    half = output_grad.shape[1] // 2
 
     def owned(piece, count):
         return jnp.concatenate([piece[:half, :count], piece[half:, :count]], axis=1).astype(F32)

time: 483 us -> 465 us (0.963)
  other arithmetic: 54.4 us -> 38.2 us
  Pallas kernels: 330 us -> 320 us
  local copies, waits for them, and re-layouts: 21.2 us -> 31 us
    unnamed x145 -> x135, local copies, waits for them, and re-layouts: 6.84 us -> 16.3 us
    pallas_call x6 -> x5, Pallas kernels: 292 us -> 283 us  [the longest x1 175 us: sum_pool(): pl.pallas_call(functools.partial(pool_kernel, plan, places, len(factors),...]
    convert_element_type x2 -> x0, other arithmetic: 7.57 us -> none  [the longest x1 5.69 us: middle_grad(): return (residual_grad, residual_grad.astype(BF16), gain_grad)]
    reduce_sum x3 -> x1, other arithmetic: 7.23 us -> 0.77 us  [local(): jnp.mean(unit_grad * own['unit'], axis=-1, keepdims=True)]
    ppermute x2, waiting for transfers between devices: 7.76 us -> 1.31 us  [swap_shared(): shared = lax.ppermute(came, 'rep', [(i, i ^ 1 << b) for i in range(n_rep)])]
    reduce_sum x2 -> x1, other arithmetic: 6.32 us -> 0.3 us  [rms_scale(): jnp.mean(values * values, axis=-1, keepdims=True) + EPSILON]
  transfers between devices with their start and end apart: 13 -> 13, of which waited for: 7 -> 5; matrix products, arithmetic and copies ran while one was open for 9% -> 10% of each run, Pallas kernels for 26% -> 27%
where the time goes in v1:
time: 465 us; the launch traced here: 458 us
  Pallas kernels  320 us (69%)
  waiting for transfers between devices  49.2 us (11%)
  other arithmetic  38.2 us (8%)
  local copies, waits for them, and re-layouts  31 us (7%)
  starting transfers between devices  11.6 us (2%)
  matrix products  6.9 us (1%)
    pallas_call x1, Pallas kernels, sum_pool(): pl.pallas_call(functools.partial(pool_kernel, plan, places, len(factors),...  175 us
    pallas_call x2, Pallas kernels, ffn(): pl.pallas_call(ffn_kernel, grid=(units // block,), out_shape=(jax.ShapeDt...  61.8 us
    ppermute x11, waiting for transfers between devices, swap(): return lax.ppermute(x, 'grp', [(0, 1), (1, 0)])  47.9 us
    pallas_call x2, Pallas kernels, back(): pl.pallas_call(back_kernel, out_shape=(jax.ShapeDtypeStruct((rows, width)...  45.6 us
    pallas_call x2, Pallas kernels, front(): pl.pallas_call(front_kernel, out_shape=(jax.ShapeDtypeStruct((rows, width...  34 us
    unnamed x135, local copies, waits for them, and re-layouts  16.3 us
  transfers between devices with their start and end apart: 13, of which 5 were waited for; matrix products, arithmetic and copies ran while one was open for 10% of the time, Pallas kernels for 27%

profile of v1, /device:TPU:9, one launch (start us, length us, event | category | flops | bytes accessed | tf_op | source)
XLA Modules:
  0.0 458.5 jit_solution(18122912498857460609)
XLA Ops:
  1.8 2.2 constant_dynamic-slice_fusion.4
  8.2 1.4 fusion.32
  9.7 8.8 %collective-permute-done.1 = bf16[96,3008]{1,0:T(8,128)(2,1)} collective-permute-done((bf16[96,3008]{1,0:T(8,128)(2,1)S(1)}, bf16[96,3008]{1,0:T(8,128)(2,1)}, u32[]{:S(2)}, u32[]{:S(2)}) %collective-permute-start.1) | collective-permute-done | bytes 577568 | tf_op jit(solution)/shard_map/ppermute | solution.py:49
  18.5 1.6 collective-permute-start.2
  26.9 17.1 %shard_map.254 = (bf16[768,768]{1,0:T(8,128)(2,1)S(1)}, bf16[768,768]{1,0:T(8,128)(2,1)S(1)}, bf16[768,128]{1,0:T(8,128)(2,1)S(1)}, bf16[768,128]{1,0:T(8,128)(2...) custom-call(bf16[768,768]{1,0:T(8,128)(2,1)} %tokens.5, f32[1,768]{1,0:T(1,128)S(1)} %get-tuple-element.153.gain, ...), custom_call_target="tpu_custom_call" | custom-call | flops 36238786560 | bytes 47185920 | tf_op jit(solution)/shard_map/pallas_call | solution.py:448
  50.0 1.4 fusion.33
  53.1 2.2 broadcast_select_fusion.3
  56.8 2.1 shard_map.255
  59.0 1.4 copy-done.15
  60.8 16.8 %shard_map.256 = (bf16[768,768]{1,0:T(8,128)(2,1)S(1)}, bf16[768,768]{1,0:T(8,128)(2,1)S(1)}, bf16[768,128]{1,0:T(8,128)(2,1)S(1)}, bf16[768,128]{1,0:T(8,128)(2...) custom-call(bf16[768,768]{1,0:T(8,128)(2,1)} %collective-permute-done.4.tokens, ...), custom_call_target="tpu_custom_call" | custom-call | flops 36238786560 | bytes 47185920 | tf_op jit(solution)/shard_map/pallas_call | solution.py:448
  77.7 4.5 broadcast_select_fusion.1
  82.2 2.1 maximum_bitcast_fusion
  84.3 5.7 %copy.39.down = bf16[2240,768]{1,0:T(8,128)(2,1)} copy(bf16[2240,768]{0,1:T(8,128)(2,1)} %maximum_bitcast_fusion) | data formatting | bytes 6881280 | tf_op jit(solution)/shard_map/transpose | solution.py:618
  92.4 1.4 copy-done.16
  94.7 7.6 %collective-permute-done.7.came = bf16[768,768]{1,0:T(8,128)(2,1)} collective-permute-done((bf16[768,768]{1,0:T(8,128)(2,1)}, bf16[768,768]{1,0:T(8,128)(2,1)}, u32[]{:S(2)}, u32[]{:S(2)}) %collective-permute-start.7) | collective-permute-done | bytes 1179680 | tf_op jit(solution)/shard_map/ppermute | solution.py:49
  102.3 30.8 %shard_map.259 = (f32[768,768]{1,0:T(8,128)}, bf16[768,768]{1,0:T(8,128)(2,1)}, bf16[2240,768]{1,0:T(8,128)(2,1)}, bf16[2240,768]{1,0:T(8,128)(2,1)}, bf16[2240,...) custom-call(bf16[768,768]{1,0:T(8,128)(2,1)} %collective-permute-done.4.tokens, ...), custom_call_target="tpu_custom_call" | custom-call | flops 15854469120 | bytes 20643840 | tf_op jit(solution)/shard_map/pallas_call | solution.py:374
  134.4 31.0 %shard_map.258 = (f32[768,768]{1,0:T(8,128)}, bf16[768,768]{1,0:T(8,128)(2,1)}, bf16[2240,768]{1,0:T(8,128)(2,1)}, bf16[2240,768]{1,0:T(8,128)(2,1)}, bf16[2240,...) custom-call(bf16[768,768]{1,0:T(8,128)(2,1)} %tokens.5, ...), custom_call_target="tpu_custom_call" | custom-call | flops 15854469120 | bytes 20643840 | tf_op jit(solution)/shard_map/pallas_call | solution.py:374
  165.4 1.4 collective-permute-start.10
  166.9 23.0 %shard_map.260 = (f32[768,768]{1,0:T(8,128)}, bf16[768,768]{1,0:T(8,128)(2,1)S(1)}, f32[1,768]{1,0:T(1,128)S(1)}, f32[1,768]{1,0:T(1,128)S(1)}, bf16[768,1024]{1...) custom-call(bf16[768,768]{1,0:T(8,128)(2,1)S(1)} %copy-done.1, ...), custom_call_target="tpu_custom_call" | custom-call | flops 54358179840 | bytes 47185920 | tf_op jit(solution)/shard_map/pallas_call | solution.py:549
  191.3 22.6 %shard_map.261 = (f32[768,768]{1,0:T(8,128)}, bf16[768,768]{1,0:T(8,128)(2,1)S(1)}, f32[1,768]{1,0:T(1,128)S(1)}, f32[1,768]{1,0:T(1,128)S(1)}, bf16[768,1024]{1...) custom-call(bf16[768,768]{1,0:T(8,128)(2,1)} %collective-permute-done.4.tokens, ...), custom_call_target="tpu_custom_call" | custom-call | flops 54358179840 | bytes 47185920 | tf_op jit(solution)/shard_map/pallas_call | solution.py:549
  213.9 3.1 fusion.26.refs_6_
  217.7 3.8 fusion.21.refs_7_
  221.5 175.3 %shard_map.262 = (bf16[768,2304]{1,0:T(8,128)(2,1)}, bf16[2240,768]{1,0:T(8,128)(2,1)}, bf16[2240,768]{1,0:T(8,128)(2,1)}, bf16[768,768]{1,0:T(8,128)(2,1)}, bf1...) custom-call(bf16[2240,768]{1,0:T(8,128)(2,1)} %get-tuple-element.106.refs_0_, ...), custom_call_target="tpu_custom_call" | custom-call | tf_op jit(solution)/shard_map/pallas_call | solution.py:300
  400.1 2.3 fusion.45
  403.7 1.6 convert_element_type.66
  406.9 3.4 convert_element_type.70
  410.3 3.4 convert_element_type.71
  414.9 1.7 maximum_convert_fusion.1
  416.6 3.7 maximum_convert_fusion
  420.3 31.2 %collective-permute-done.12 = bf16[768,768]{1,0:T(8,128)(2,1)S(1)} collective-permute-done((bf16[768,768]{1,0:T(8,128)(2,1)}, bf16[768,768]{1,0:T(8,128)(2,1)S(1)}, u32[]{:S(2)}, u32[]{:S(2)}) %collective-permute-start.12) | collective-permute-done | bytes 1179680 | tf_op jit(solution)/shard_map/ppermute | solution.py:49
  453.9 1.9 convert_add_fusion
  456.1 2.2 fusion.9
  (199 shorter events, 38.1 us)
Async XLA Ops:
  4.1 14.4 %collective-permute-start.1 = (bf16[96,3008]{1,0:T(8,128)(2,1)S(1)}, bf16[96,3008]{1,0:T(8,128)(2,1)}, u32[]{:S(2)}, u32[]{:S(2)}) collective-permute-start(bf16[96,3008]{1,0:T(8,128)(2,1)S(1)} %fusion.31), channel_id=1, source_target_pairs={{0,1},{1,0},{2,3},{3,2},{4,5},{5,4},{6,7},{7,6},{8,9},{9,8},{10,11... | collective-permute-start | bytes 1732616 | tf_op jit(solution)/shard_map/ppermute | solution.py:49
  5.4 15.1 %collective-permute-start = (bf16[2,384]{1,0:T(2,128)(2,1)S(1)}, bf16[2,384]{1,0:T(2,128)(2,1)S(1)}, u32[]{:S(2)}, u32[]{:S(2)}) collective-permute-start(bf16[2,384]{1,0:T(2,128)(2,1)S(1)} %pad_maximum_fusion.8), channel_id=1, source_target_pairs={{0,1},{1,0},{2,3},{3,2},{4,5},{5,4},{6,7},{7,6},{8,9},{9,8},{10,11... | collective-permute-start | bytes 4616 | tf_op jit(solution)/shard_map/ppermute | solution.py:49
  6.0 43.3 %collective-permute-start.5 = (s32[1,4]{1,0:T(1,128)S(1)}, s32[1,4]{1,0:T(1,128)S(1)}, u32[]{:S(2)}, u32[]{:S(2)}) collective-permute-start(s32[1,4]{1,0:T(1,128)S(1)} %copy-done.64), channel_id=1, source_target_pairs={{0,1},{1,0},{2,3},{3,2},{4,5},{5,4},{6,7},{7,6},{8,9},{9,8},{10,11... | collective-permute-start | bytes 56 | tf_op jit(solution)/shard_map/ppermute | solution.py:49
  7.3 13.2 %copy-start.56 = (bf16[768]{0:T(1024)(128)(2,1)S(1)}, bf16[768]{0:T(1024)(128)(2,1)}, u32[]{:S(2)}) copy-start(bf16[768]{0:T(1024)(128)(2,1)} %param.19) | copy-start | bytes 4612
  18.5 4.5 collective-permute-start.2
  21.8 30.1 %collective-permute-start.4 = (bf16[768,768]{1,0:T(8,128)(2,1)S(1)}, bf16[768,768]{1,0:T(8,128)(2,1)}, u32[]{:S(2)}, u32[]{:S(2)}) collective-permute-start(bf16[768,768]{1,0:T(8,128)(2,1)S(1)} %copy-done), channel_id=1, source_target_pairs={{0,1},{1,0},{2,3},{3,2},{4,5},{5,4},{6,7},{7,6},{8,9},{9,8},{10,11... | collective-permute-start | bytes 3538952 | tf_op jit(solution)/shard_map/ppermute | solution.py:49
  25.6 27.6 %collective-permute-start.3 = (bf16[192,3008]{1,0:T(8,128)(2,1)}, bf16[192,3008]{1,0:T(8,128)(2,1)}, u32[]{:S(2)}, u32[]{:S(2)}) collective-permute-start(bf16[192,3008]{1,0:T(8,128)(2,1)} %pad_maximum_fusion.1), channel_id=1, source_target_pairs={{0,4},{2,6},{4,0},{6,2},{8,12},{10,14},{12,8},{14,10},{16,20},{18,... | collective-permute-start | bytes 3465224 | tf_op jit(solution)/shard_map/ppermute | solution.py:62
  49.7 45.1 %collective-permute-start.8 = (bf16[768,768]{1,0:T(8,128)(2,1)}, bf16[768,768]{1,0:T(8,128)(2,1)}, u32[]{:S(2)}, u32[]{:S(2)}) collective-permute-start(bf16[768,768]{1,0:T(8,128)(2,1)} %refs_9_.1), channel_id=1, source_target_pairs={{0,1},{1,0},{2,3},{3,2},{4,5},{5,4},{6,7},{7,6},{8,9},{9,8},{10,11... | collective-permute-start | bytes 3538952 | tf_op jit(solution)/shard_map/ppermute | solution.py:49
  56.8 33.1 %copy-start.2 = (bf16[768,768]{1,0:T(8,128)(2,1)}, bf16[768,768]{1,0:T(8,128)(2,1)S(1)}, u32[]{:S(2)}) copy-start(bf16[768,768]{1,0:T(8,128)(2,1)S(1)} %pad_maximum_fusion.2.ow) | copy-start | bytes 3538948
  60.4 41.9 %collective-permute-start.7 = (bf16[768,768]{1,0:T(8,128)(2,1)}, bf16[768,768]{1,0:T(8,128)(2,1)}, u32[]{:S(2)}, u32[]{:S(2)}) collective-permute-start(bf16[768,768]{1,0:T(8,128)(2,1)} %get-tuple-element.81), channel_id=1, source_target_pairs={{0,1},{1,0},{2,3},{3,2},{4,5},{5,4},{6,7},{7,6},{8,9},{9,8},{10,11... | collective-permute-start | bytes 3538952 | tf_op jit(solution)/shard_map/ppermute | solution.py:49
  93.8 39.6 %collective-permute-start.6 = (bf16[768,768]{1,0:T(8,128)(2,1)S(1)}, bf16[768,768]{1,0:T(8,128)(2,1)S(1)}, u32[]{:S(2)}, u32[]{:S(2)}) collective-permute-start(bf16[768,768]{1,0:T(8,128)(2,1)S(1)} %get-tuple-element.82), channel_id=1, source_target_pairs={{0,1},{1,0},{2,3},{3,2},{4,5},{5,4},{6,7},{7,6},{8,9},{9,8},{10,11... | collective-permute-start | bytes 3538952 | tf_op jit(solution)/shard_map/ppermute | solution.py:49
  133.1 32.2 %collective-permute-start.9 = (bf16[768,768]{1,0:T(8,128)(2,1)}, bf16[768,768]{1,0:T(8,128)(2,1)S(1)}, u32[]{:S(2)}, u32[]{:S(2)}) collective-permute-start(bf16[768,768]{1,0:T(8,128)(2,1)} %get-tuple-element.89), channel_id=1, source_target_pairs={{0,1},{1,0},{2,3},{3,2},{4,5},{5,4},{6,7},{7,6},{8,9},{9,8},{10,11... | collective-permute-start | bytes 3538952 | tf_op jit(solution)/shard_map/ppermute | solution.py:49
  134.3 32.4 %copy-start.1 = (bf16[768,768]{1,0:T(8,128)(2,1)S(1)}, bf16[768,768]{1,0:T(8,128)(2,1)}, u32[]{:S(2)}) copy-start(bf16[768,768]{1,0:T(8,128)(2,1)} %tokens.5) | copy-start | bytes 3538948
  134.3 32.4 %copy-start.8 = (f32[768,128]{1,0:T(8,128)S(1)}, f32[768,128]{1,0:T(8,128)}, u32[]{:S(2)}) copy-start(f32[768,128]{1,0:T(8,128)} %copy-done.7) | copy-start | bytes 1179652
  134.3 32.4 %copy-start.10 = (f32[768,128]{1,0:T(8,128)S(1)}, f32[768,128]{1,0:T(8,128)}, u32[]{:S(2)}) copy-start(f32[768,128]{1,0:T(8,128)} %copy-done.9) | copy-start | bytes 1179652
  134.3 32.4 %copy-start.11 = (f32[1,768]{1,0:T(1,128)S(1)}, f32[1,768]{1,0:T(1,128)}, u32[]{:S(2)}) copy-start(f32[1,768]{1,0:T(1,128)} %get-tuple-element.152.gain) | copy-start | bytes 9220
  134.3 32.4 %copy-start.30 = (f32[768,128]{1,0:T(8,128)S(1)}, f32[768,128]{1,0:T(8,128)}, u32[]{:S(2)}) copy-start(f32[768,128]{1,0:T(8,128)} %copy-done.29) | copy-start | bytes 1179652
  134.4 32.4 %copy-start.34 = (bf16[768,128]{1,0:T(8,128)(2,1)S(1)}, bf16[768,128]{1,0:T(8,128)(2,1)}, u32[]{:S(2)}) copy-start(bf16[768,128]{1,0:T(8,128)(2,1)} %copy-done.33) | copy-start | bytes 589828
  134.4 32.4 %copy-start.36 = (bf16[768,128]{1,0:T(8,128)(2,1)S(1)}, bf16[768,128]{1,0:T(8,128)(2,1)}, u32[]{:S(2)}) copy-start(bf16[768,128]{1,0:T(8,128)(2,1)} %copy-done.35) | copy-start | bytes 589828
  165.4 24.9 %collective-permute-start.10 = (bf16[768,768]{1,0:T(8,128)(2,1)}, bf16[768,768]{1,0:T(8,128)(2,1)S(1)}, u32[]{:S(2)}, u32[]{:S(2)}) collective-permute-start(bf16[768,768]{1,0:T(8,128)(2,1)} %get-tuple-element.90), channel_id=1, source_target_pairs={{0,1},{1,0},{2,3},{3,2},{4,5},{5,4},{6,7},{7,6},{8,9},{9,8},{10,11... | collective-permute-start | bytes 3538952 | tf_op jit(solution)/shard_map/ppermute | solution.py:49
  166.8 24.5 %copy-start.4 = (f32[768,128]{1,0:T(8,128)S(1)}, f32[768,128]{1,0:T(8,128)}, u32[]{:S(2)}) copy-start(f32[768,128]{1,0:T(8,128)} %copy-done.3) | copy-start | bytes 1179652
  166.8 24.5 %copy-start.6 = (f32[768,128]{1,0:T(8,128)S(1)}, f32[768,128]{1,0:T(8,128)}, u32[]{:S(2)}) copy-start(f32[768,128]{1,0:T(8,128)} %copy-done.5) | copy-start | bytes 1179652
  166.8 24.4 %copy-start.32 = (f32[768,128]{1,0:T(8,128)S(1)}, f32[768,128]{1,0:T(8,128)}, u32[]{:S(2)}) copy-start(f32[768,128]{1,0:T(8,128)} %copy-done.31) | copy-start | bytes 1179652
  166.9 24.4 %copy-start.38 = (bf16[768,128]{1,0:T(8,128)(2,1)S(1)}, bf16[768,128]{1,0:T(8,128)(2,1)}, u32[]{:S(2)}) copy-start(bf16[768,128]{1,0:T(8,128)(2,1)} %copy-done.37) | copy-start | bytes 589828
  166.9 24.4 %copy-start.40 = (bf16[768,128]{1,0:T(8,128)(2,1)S(1)}, bf16[768,128]{1,0:T(8,128)(2,1)}, u32[]{:S(2)}) copy-start(bf16[768,128]{1,0:T(8,128)(2,1)} %copy-done.39) | copy-start | bytes 589828
  191.3 22.6 %copy-start.19 = (bf16[768,768]{1,0:T(8,128)(2,1)S(1)}, bf16[768,768]{1,0:T(8,128)(2,1)}, u32[]{:S(2)}) copy-start(bf16[768,768]{1,0:T(8,128)(2,1)} %copy-done.17) | copy-start | bytes 3538948
  191.3 22.6 %copy-start.22 = (bf16[768,768]{1,0:T(8,128)(2,1)S(1)}, bf16[768,768]{1,0:T(8,128)(2,1)}, u32[]{:S(2)}) copy-start(bf16[768,768]{1,0:T(8,128)(2,1)} %copy-done.20) | copy-start | bytes 3538948
  398.7 53.7 %collective-permute-start.11 = (bf16[768,768]{1,0:T(8,128)(2,1)}, bf16[768,768]{1,0:T(8,128)(2,1)S(1)}, u32[]{:S(2)}, u32[]{:S(2)}) collective-permute-start(bf16[768,768]{1,0:T(8,128)(2,1)} %get-tuple-element.91), channel_id=1, source_target_pairs={{0,1},{1,0},{2,3},{3,2},{4,5},{5,4},{6,7},{7,6},{8,9},{9,8},{10,11... | collective-permute-start | bytes 3538952 | tf_op jit(solution)/shard_map/ppermute | solution.py:49
  400.0 51.6 %collective-permute-start.12 = (bf16[768,768]{1,0:T(8,128)(2,1)}, bf16[768,768]{1,0:T(8,128)(2,1)S(1)}, u32[]{:S(2)}, u32[]{:S(2)}) collective-permute-start(bf16[768,768]{1,0:T(8,128)(2,1)} %copy-done.12), channel_id=1, source_target_pairs={{0,1},{1,0},{2,3},{3,2},{4,5},{5,4},{6,7},{7,6},{8,9},{9,8},{10,11... | collective-permute-start | bytes 3538952 | tf_op jit(solution)/shard_map/ppermute | solution.py:49
  416.6 34.9 %copy-start.41 = (f32[768,768]{1,0:T(8,128)S(1)}, f32[768,768]{1,0:T(8,128)}, u32[]{:S(2)}) copy-start(f32[768,768]{1,0:T(8,128)} %get-tuple-element.98) | copy-start | bytes 7077892
  416.6 34.9 %copy-start.54 = (f32[768]{0:T(1024)S(1)}, f32[768]{0:T(1024)}, u32[]{:S(2)}) copy-start(f32[768]{0:T(1024)} %add_rsqrt_fusion) | copy-start | bytes 9220
  416.6 34.9 %copy-start.55 = (f32[768]{0:T(1024)S(1)}, f32[768]{0:T(1024)}, u32[]{:S(2)}) copy-start(f32[768]{0:T(1024)} %get-tuple-element.151) | copy-start | bytes 9220
  (48 other events, 147.3 us)

commit v2 on v1

--- a/solution.py
+++ b/solution.py
@@ -138,8 +138,13 @@
         for copy in waits:
             copy.wait()
         first, second = makers[group][1]
-        product = mm_nn(lefts[k % slots, 0, :count, :], first[...]) + mm_nn(lefts[k % slots, 1, :count, :], second[...])
-        pool[pl.ds(start, count), :] = product.astype(BF16)
+
+        def one(i, step):
+            rows = pl.ds(pl.multiple_of(i, 16), step)
+            product = mm_nn(lefts[k % slots, 0, rows, :], first[...]) + mm_nn(lefts[k % slots, 1, rows, :], second[...])
+            pool[pl.ds(pl.multiple_of(start + i, 16), step), :] = product.astype(BF16)
+
+        rows_loop(count, count // 2 if count % 32 == 0 else count, one)
         fetch(k + slots)
 
     for k in range(slots):
@@ -639,7 +644,7 @@
     came_other = swap(part_own_b)
     oth = begin(after(tokens_other, own["kept"][0]), after(lengths_other, own["kept"][0]))
     oth["part"], part_oth_b = project(oth["kept"][0], output_cols)
-    came_own = swap(after(part_oth_b, part_own_b))
+    came_own = swap(after(part_oth_b, came_other))
 
     def middle(kept, came, cot, part_type):
         residual, normed, *wide, grad, grad_b, part = ffn(

time: 465 us -> 466 us (level)
  no operation moved by 1% of the time
where the time goes in v2:
time: 466 us; the launch traced here: 459 us
  Pallas kernels  318 us (68%)
  waiting for transfers between devices  51.7 us (11%)
  other arithmetic  38.2 us (8%)
  local copies, waits for them, and re-layouts  31.8 us (7%)
  starting transfers between devices  10.7 us (2%)
  matrix products  6.91 us (1%)
    pallas_call x1, Pallas kernels, sum_pool(): pl.pallas_call(functools.partial(pool_kernel, plan, places, len(factors),...  174 us
    pallas_call x2, Pallas kernels, ffn(): pl.pallas_call(ffn_kernel, grid=(units // block,), out_shape=(jax.ShapeDt...  61.7 us
    ppermute x11, waiting for transfers between devices, swap(): return lax.ppermute(x, 'grp', [(0, 1), (1, 0)])  50.2 us
    pallas_call x2, Pallas kernels, back(): pl.pallas_call(back_kernel, out_shape=(jax.ShapeDtypeStruct((rows, width)...  45.6 us
    pallas_call x2, Pallas kernels, front(): pl.pallas_call(front_kernel, out_shape=(jax.ShapeDtypeStruct((rows, width...  33.8 us
    unnamed x135, local copies, waits for them, and re-layouts  17.1 us
  transfers between devices with their start and end apart: 13, of which 5 were waited for; matrix products, arithmetic and copies ran while one was open for 10% of the time, Pallas kernels for 27%

profile of v2, /device:TPU:9, one launch (start us, length us, event | category | flops | bytes accessed | tf_op | source)
XLA Modules:
  0.0 459.3 jit_solution(9309978186593102700)
XLA Ops:
  1.8 2.2 constant_dynamic-slice_fusion.4
  8.2 1.4 fusion.32
  9.7 8.8 %collective-permute-done.1 = bf16[96,3008]{1,0:T(8,128)(2,1)} collective-permute-done((bf16[96,3008]{1,0:T(8,128)(2,1)S(1)}, bf16[96,3008]{1,0:T(8,128)(2,1)}, u32[]{:S(2)}, u32[]{:S(2)}) %collective-permute-start.1) | collective-permute-done | bytes 577568 | tf_op jit(solution)/shard_map/ppermute | solution.py:49
  18.5 1.6 collective-permute-start.2
  26.9 17.0 %shard_map.254 = (bf16[768,768]{1,0:T(8,128)(2,1)S(1)}, bf16[768,768]{1,0:T(8,128)(2,1)S(1)}, bf16[768,128]{1,0:T(8,128)(2,1)S(1)}, bf16[768,128]{1,0:T(8,128)(2...) custom-call(bf16[768,768]{1,0:T(8,128)(2,1)} %tokens.5, f32[1,768]{1,0:T(1,128)S(1)} %get-tuple-element.153.gain, ...), custom_call_target="tpu_custom_call" | custom-call | flops 36238786560 | bytes 47185920 | tf_op jit(solution)/shard_map/pallas_call | solution.py:453
  49.9 1.4 fusion.33
  51.7 1.4 collective-permute-done.3
  53.1 2.2 broadcast_select_fusion.3
  56.8 2.1 shard_map.255
  60.7 16.8 %shard_map.256 = (bf16[768,768]{1,0:T(8,128)(2,1)S(1)}, bf16[768,768]{1,0:T(8,128)(2,1)S(1)}, bf16[768,128]{1,0:T(8,128)(2,1)S(1)}, bf16[768,128]{1,0:T(8,128)(2...) custom-call(bf16[768,768]{1,0:T(8,128)(2,1)} %collective-permute-done.4.tokens, ...), custom_call_target="tpu_custom_call" | custom-call | flops 36238786560 | bytes 47185920 | tf_op jit(solution)/shard_map/pallas_call | solution.py:453
  77.6 4.5 broadcast_select_fusion.1
  82.1 2.1 maximum_bitcast_fusion
  84.1 5.7 %copy.39.down = bf16[2240,768]{1,0:T(8,128)(2,1)} copy(bf16[2240,768]{0,1:T(8,128)(2,1)} %maximum_bitcast_fusion) | data formatting | bytes 6881280 | tf_op jit(solution)/shard_map/transpose | solution.py:623
  93.7 8.5 %collective-permute-done.6.came = bf16[768,768]{1,0:T(8,128)(2,1)} collective-permute-done((bf16[768,768]{1,0:T(8,128)(2,1)}, bf16[768,768]{1,0:T(8,128)(2,1)}, u32[]{:S(2)}, u32[]{:S(2)}) %collective-permute-start.6) | collective-permute-done | bytes 1179680 | tf_op jit(solution)/shard_map/ppermute | solution.py:49
  102.3 30.5 %shard_map.259 = (f32[768,768]{1,0:T(8,128)}, bf16[768,768]{1,0:T(8,128)(2,1)}, bf16[2240,768]{1,0:T(8,128)(2,1)}, bf16[2240,768]{1,0:T(8,128)(2,1)}, bf16[2240,...) custom-call(bf16[768,768]{1,0:T(8,128)(2,1)} %collective-permute-done.4.tokens, ...), custom_call_target="tpu_custom_call" | custom-call | flops 15854469120 | bytes 20643840 | tf_op jit(solution)/shard_map/pallas_call | solution.py:379
  135.3 31.2 %shard_map.258 = (f32[768,768]{1,0:T(8,128)}, bf16[768,768]{1,0:T(8,128)(2,1)}, bf16[2240,768]{1,0:T(8,128)(2,1)}, bf16[2240,768]{1,0:T(8,128)(2,1)}, bf16[2240,...) custom-call(bf16[768,768]{1,0:T(8,128)(2,1)} %tokens.5, ...), custom_call_target="tpu_custom_call" | custom-call | flops 15854469120 | bytes 20643840 | tf_op jit(solution)/shard_map/pallas_call | solution.py:379
  167.6 23.0 %shard_map.260 = (f32[768,768]{1,0:T(8,128)}, bf16[768,768]{1,0:T(8,128)(2,1)S(1)}, f32[1,768]{1,0:T(1,128)S(1)}, f32[1,768]{1,0:T(1,128)S(1)}, bf16[768,1024]{1...) custom-call(bf16[768,768]{1,0:T(8,128)(2,1)S(1)} %copy-done.1, ...), custom_call_target="tpu_custom_call" | custom-call | flops 54358179840 | bytes 47185920 | tf_op jit(solution)/shard_map/pallas_call | solution.py:554
  190.6 1.7 collective-permute-done.10.came
  193.4 22.5 %shard_map.261 = (f32[768,768]{1,0:T(8,128)}, bf16[768,768]{1,0:T(8,128)(2,1)S(1)}, f32[1,768]{1,0:T(1,128)S(1)}, f32[1,768]{1,0:T(1,128)S(1)}, bf16[768,1024]{1...) custom-call(bf16[768,768]{1,0:T(8,128)(2,1)} %collective-permute-done.4.tokens, ...), custom_call_target="tpu_custom_call" | custom-call | flops 54358179840 | bytes 47185920 | tf_op jit(solution)/shard_map/pallas_call | solution.py:554
  216.0 3.1 fusion.26.refs_6_
  219.7 3.8 fusion.21.refs_7_
  223.5 174.0 %shard_map.262 = (bf16[768,2304]{1,0:T(8,128)(2,1)}, bf16[2240,768]{1,0:T(8,128)(2,1)}, bf16[2240,768]{1,0:T(8,128)(2,1)}, bf16[768,768]{1,0:T(8,128)(2,1)}, bf1...) custom-call(bf16[2240,768]{1,0:T(8,128)(2,1)} %get-tuple-element.106.refs_0_, ...), custom_call_target="tpu_custom_call" | custom-call | tf_op jit(solution)/shard_map/pallas_call | solution.py:305
  399.5 1.5 collective-permute-start.12
  400.9 2.3 fusion.45
  404.6 1.6 convert_element_type.66
  407.7 3.4 convert_element_type.70
  411.1 3.4 convert_element_type.71
  415.7 1.7 maximum_convert_fusion.1
  417.4 3.7 maximum_convert_fusion
  421.1 31.2 %collective-permute-done.12 = bf16[768,768]{1,0:T(8,128)(2,1)S(1)} collective-permute-done((bf16[768,768]{1,0:T(8,128)(2,1)}, bf16[768,768]{1,0:T(8,128)(2,1)S(1)}, u32[]{:S(2)}, u32[]{:S(2)}) %collective-permute-start.12) | collective-permute-done | bytes 1179680 | tf_op jit(solution)/shard_map/ppermute | solution.py:49
  454.7 1.9 convert_add_fusion
  456.9 2.2 fusion.9
  (199 shorter events, 39.1 us)
Async XLA Ops:
  4.1 14.4 %collective-permute-start.1 = (bf16[96,3008]{1,0:T(8,128)(2,1)S(1)}, bf16[96,3008]{1,0:T(8,128)(2,1)}, u32[]{:S(2)}, u32[]{:S(2)}) collective-permute-start(bf16[96,3008]{1,0:T(8,128)(2,1)S(1)} %fusion.31), channel_id=1, source_target_pairs={{0,1},{1,0},{2,3},{3,2},{4,5},{5,4},{6,7},{7,6},{8,9},{9,8},{10,11... | collective-permute-start | bytes 1732616 | tf_op jit(solution)/shard_map/ppermute | solution.py:49
  5.4 15.1 %collective-permute-start = (bf16[2,384]{1,0:T(2,128)(2,1)S(1)}, bf16[2,384]{1,0:T(2,128)(2,1)S(1)}, u32[]{:S(2)}, u32[]{:S(2)}) collective-permute-start(bf16[2,384]{1,0:T(2,128)(2,1)S(1)} %pad_maximum_fusion.8), channel_id=1, source_target_pairs={{0,1},{1,0},{2,3},{3,2},{4,5},{5,4},{6,7},{7,6},{8,9},{9,8},{10,11... | collective-permute-start | bytes 4616 | tf_op jit(solution)/shard_map/ppermute | solution.py:49
  6.0 43.2 %collective-permute-start.5 = (s32[1,4]{1,0:T(1,128)S(1)}, s32[1,4]{1,0:T(1,128)S(1)}, u32[]{:S(2)}, u32[]{:S(2)}) collective-permute-start(s32[1,4]{1,0:T(1,128)S(1)} %copy-done.64), channel_id=1, source_target_pairs={{0,1},{1,0},{2,3},{3,2},{4,5},{5,4},{6,7},{7,6},{8,9},{9,8},{10,11... | collective-permute-start | bytes 56 | tf_op jit(solution)/shard_map/ppermute | solution.py:49
  7.3 13.2 %copy-start.56 = (bf16[768]{0:T(1024)(128)(2,1)S(1)}, bf16[768]{0:T(1024)(128)(2,1)}, u32[]{:S(2)}) copy-start(bf16[768]{0:T(1024)(128)(2,1)} %param.19) | copy-start | bytes 4612
  18.5 4.5 collective-permute-start.2
  21.8 29.9 %collective-permute-start.4 = (bf16[768,768]{1,0:T(8,128)(2,1)S(1)}, bf16[768,768]{1,0:T(8,128)(2,1)}, u32[]{:S(2)}, u32[]{:S(2)}) collective-permute-start(bf16[768,768]{1,0:T(8,128)(2,1)S(1)} %copy-done), channel_id=1, source_target_pairs={{0,1},{1,0},{2,3},{3,2},{4,5},{5,4},{6,7},{7,6},{8,9},{9,8},{10,11... | collective-permute-start | bytes 3538952 | tf_op jit(solution)/shard_map/ppermute | solution.py:49
  25.6 27.6 %collective-permute-start.3 = (bf16[192,3008]{1,0:T(8,128)(2,1)}, bf16[192,3008]{1,0:T(8,128)(2,1)}, u32[]{:S(2)}, u32[]{:S(2)}) collective-permute-start(bf16[192,3008]{1,0:T(8,128)(2,1)} %pad_maximum_fusion.1), channel_id=1, source_target_pairs={{0,4},{2,6},{4,0},{6,2},{8,12},{10,14},{12,8},{14,10},{16,20},{18,... | collective-permute-start | bytes 3465224 | tf_op jit(solution)/shard_map/ppermute | solution.py:62
  49.6 52.8 %collective-permute-start.8 = (bf16[768,768]{1,0:T(8,128)(2,1)}, bf16[768,768]{1,0:T(8,128)(2,1)}, u32[]{:S(2)}, u32[]{:S(2)}) collective-permute-start(bf16[768,768]{1,0:T(8,128)(2,1)} %refs_9_.1), channel_id=1, source_target_pairs={{0,1},{1,0},{2,3},{3,2},{4,5},{5,4},{6,7},{7,6},{8,9},{9,8},{10,11... | collective-permute-start | bytes 3538952 | tf_op jit(solution)/shard_map/ppermute | solution.py:49
  56.8 33.0 %copy-start.2 = (bf16[768,768]{1,0:T(8,128)(2,1)}, bf16[768,768]{1,0:T(8,128)(2,1)S(1)}, u32[]{:S(2)}) copy-start(bf16[768,768]{1,0:T(8,128)(2,1)S(1)} %pad_maximum_fusion.2.ow) | copy-start | bytes 3538948
  60.4 41.8 %collective-permute-start.6 = (bf16[768,768]{1,0:T(8,128)(2,1)}, bf16[768,768]{1,0:T(8,128)(2,1)}, u32[]{:S(2)}, u32[]{:S(2)}) collective-permute-start(bf16[768,768]{1,0:T(8,128)(2,1)} %get-tuple-element.81), channel_id=1, source_target_pairs={{0,1},{1,0},{2,3},{3,2},{4,5},{5,4},{6,7},{7,6},{8,9},{9,8},{10,11... | collective-permute-start | bytes 3538952 | tf_op jit(solution)/shard_map/ppermute | solution.py:49
  102.2 32.0 %collective-permute-start.7 = (bf16[768,768]{1,0:T(8,128)(2,1)S(1)}, bf16[768,768]{1,0:T(8,128)(2,1)S(1)}, u32[]{:S(2)}, u32[]{:S(2)}) collective-permute-start(bf16[768,768]{1,0:T(8,128)(2,1)S(1)} %get-tuple-element.82), channel_id=1, source_target_pairs={{0,1},{1,0},{2,3},{3,2},{4,5},{5,4},{6,7},{7,6},{8,9},{9,8},{10,11... | collective-permute-start | bytes 3538952 | tf_op jit(solution)/shard_map/ppermute | solution.py:49
  132.8 33.7 %collective-permute-start.9 = (bf16[768,768]{1,0:T(8,128)(2,1)}, bf16[768,768]{1,0:T(8,128)(2,1)S(1)}, u32[]{:S(2)}, u32[]{:S(2)}) collective-permute-start(bf16[768,768]{1,0:T(8,128)(2,1)} %get-tuple-element.89), channel_id=1, source_target_pairs={{0,1},{1,0},{2,3},{3,2},{4,5},{5,4},{6,7},{7,6},{8,9},{9,8},{10,11... | collective-permute-start | bytes 3538952 | tf_op jit(solution)/shard_map/ppermute | solution.py:49
  135.2 32.3 %copy-start.1 = (bf16[768,768]{1,0:T(8,128)(2,1)S(1)}, bf16[768,768]{1,0:T(8,128)(2,1)}, u32[]{:S(2)}) copy-start(bf16[768,768]{1,0:T(8,128)(2,1)} %tokens.5) | copy-start | bytes 3538948
  135.2 32.3 %copy-start.8 = (f32[768,128]{1,0:T(8,128)S(1)}, f32[768,128]{1,0:T(8,128)}, u32[]{:S(2)}) copy-start(f32[768,128]{1,0:T(8,128)} %copy-done.7) | copy-start | bytes 1179652
  135.2 32.3 %copy-start.10 = (f32[768,128]{1,0:T(8,128)S(1)}, f32[768,128]{1,0:T(8,128)}, u32[]{:S(2)}) copy-start(f32[768,128]{1,0:T(8,128)} %copy-done.9) | copy-start | bytes 1179652
  135.3 32.3 %copy-start.11 = (f32[1,768]{1,0:T(1,128)S(1)}, f32[1,768]{1,0:T(1,128)}, u32[]{:S(2)}) copy-start(f32[1,768]{1,0:T(1,128)} %get-tuple-element.152.gain) | copy-start | bytes 9220
  135.3 32.3 %copy-start.30 = (f32[768,128]{1,0:T(8,128)S(1)}, f32[768,128]{1,0:T(8,128)}, u32[]{:S(2)}) copy-start(f32[768,128]{1,0:T(8,128)} %copy-done.29) | copy-start | bytes 1179652
  135.3 32.3 %copy-start.34 = (bf16[768,128]{1,0:T(8,128)(2,1)S(1)}, bf16[768,128]{1,0:T(8,128)(2,1)}, u32[]{:S(2)}) copy-start(bf16[768,128]{1,0:T(8,128)(2,1)} %copy-done.33) | copy-start | bytes 589828
  135.3 32.3 %copy-start.36 = (bf16[768,128]{1,0:T(8,128)(2,1)S(1)}, bf16[768,128]{1,0:T(8,128)(2,1)}, u32[]{:S(2)}) copy-start(bf16[768,128]{1,0:T(8,128)(2,1)} %copy-done.35) | copy-start | bytes 589828
  166.5 25.8 %collective-permute-start.10 = (bf16[768,768]{1,0:T(8,128)(2,1)}, bf16[768,768]{1,0:T(8,128)(2,1)S(1)}, u32[]{:S(2)}, u32[]{:S(2)}) collective-permute-start(bf16[768,768]{1,0:T(8,128)(2,1)} %get-tuple-element.90), channel_id=1, source_target_pairs={{0,1},{1,0},{2,3},{3,2},{4,5},{5,4},{6,7},{7,6},{8,9},{9,8},{10,11... | collective-permute-start | bytes 3538952 | tf_op jit(solution)/shard_map/ppermute | solution.py:49
  167.6 25.8 %copy-start.4 = (f32[768,128]{1,0:T(8,128)S(1)}, f32[768,128]{1,0:T(8,128)}, u32[]{:S(2)}) copy-start(f32[768,128]{1,0:T(8,128)} %copy-done.3) | copy-start | bytes 1179652
  167.6 25.8 %copy-start.6 = (f32[768,128]{1,0:T(8,128)S(1)}, f32[768,128]{1,0:T(8,128)}, u32[]{:S(2)}) copy-start(f32[768,128]{1,0:T(8,128)} %copy-done.5) | copy-start | bytes 1179652
  167.6 25.8 %copy-start.32 = (f32[768,128]{1,0:T(8,128)S(1)}, f32[768,128]{1,0:T(8,128)}, u32[]{:S(2)}) copy-start(f32[768,128]{1,0:T(8,128)} %copy-done.31) | copy-start | bytes 1179652
  167.6 25.8 %copy-start.38 = (bf16[768,128]{1,0:T(8,128)(2,1)S(1)}, bf16[768,128]{1,0:T(8,128)(2,1)}, u32[]{:S(2)}) copy-start(bf16[768,128]{1,0:T(8,128)(2,1)} %copy-done.37) | copy-start | bytes 589828
  167.6 25.8 %copy-start.40 = (bf16[768,128]{1,0:T(8,128)(2,1)S(1)}, bf16[768,128]{1,0:T(8,128)(2,1)}, u32[]{:S(2)}) copy-start(bf16[768,128]{1,0:T(8,128)(2,1)} %copy-done.39) | copy-start | bytes 589828
  193.4 22.5 %copy-start.19 = (bf16[768,768]{1,0:T(8,128)(2,1)S(1)}, bf16[768,768]{1,0:T(8,128)(2,1)}, u32[]{:S(2)}) copy-start(bf16[768,768]{1,0:T(8,128)(2,1)} %copy-done.17) | copy-start | bytes 3538948
  193.4 22.5 %copy-start.22 = (bf16[768,768]{1,0:T(8,128)(2,1)S(1)}, bf16[768,768]{1,0:T(8,128)(2,1)}, u32[]{:S(2)}) copy-start(bf16[768,768]{1,0:T(8,128)(2,1)} %copy-done.20) | copy-start | bytes 3538948
  399.5 53.7 %collective-permute-start.11 = (bf16[768,768]{1,0:T(8,128)(2,1)}, bf16[768,768]{1,0:T(8,128)(2,1)S(1)}, u32[]{:S(2)}, u32[]{:S(2)}) collective-permute-start(bf16[768,768]{1,0:T(8,128)(2,1)} %get-tuple-element.91), channel_id=1, source_target_pairs={{0,1},{1,0},{2,3},{3,2},{4,5},{5,4},{6,7},{7,6},{8,9},{9,8},{10,11... | collective-permute-start | bytes 3538952 | tf_op jit(solution)/shard_map/ppermute | solution.py:49
  399.5 52.9 %collective-permute-start.12 = (bf16[768,768]{1,0:T(8,128)(2,1)}, bf16[768,768]{1,0:T(8,128)(2,1)S(1)}, u32[]{:S(2)}, u32[]{:S(2)}) collective-permute-start(bf16[768,768]{1,0:T(8,128)(2,1)} %copy-done.12), channel_id=1, source_target_pairs={{0,1},{1,0},{2,3},{3,2},{4,5},{5,4},{6,7},{7,6},{8,9},{9,8},{10,11... | collective-permute-start | bytes 3538952 | tf_op jit(solution)/shard_map/ppermute | solution.py:49
  417.4 34.9 %copy-start.41 = (f32[768,768]{1,0:T(8,128)S(1)}, f32[768,768]{1,0:T(8,128)}, u32[]{:S(2)}) copy-start(f32[768,768]{1,0:T(8,128)} %get-tuple-element.98) | copy-start | bytes 7077892
  417.4 34.9 %copy-start.54 = (f32[768]{0:T(1024)S(1)}, f32[768]{0:T(1024)}, u32[]{:S(2)}) copy-start(f32[768]{0:T(1024)} %add_rsqrt_fusion) | copy-start | bytes 9220
  417.4 34.9 %copy-start.55 = (f32[768]{0:T(1024)S(1)}, f32[768]{0:T(1024)}, u32[]{:S(2)}) copy-start(f32[768]{0:T(1024)} %get-tuple-element.151) | copy-start | bytes 9220
  (48 other events, 147.0 us)
